TPU v7x, 8 devices: a whole 2x2x1 slice. The times are simulated.
8 devices in a mesh: dp: 1 (over z), tp: 8 (over y, x, core).
Axes of the slice: x: 2, y: 2, z: 1, core: 2. Of those that a mesh axis runs over, the one named last changes fastest.
Arguments:
- hidden: bfloat16 [1, 4096, 5120], P('dp', 'tp')
- attn_gain: float32 [5120], replicated
- w_q: bfloat16 [5120, 5120], P(None, 'tp')
- w_k: bfloat16 [5120, 5120], P(None, 'tp')
- w_v: bfloat16 [5120, 5120], P(None, 'tp')
- q_gain: float32 [5120], P('tp')
- k_gain: float32 [5120], P('tp')
- w_o: bfloat16 [5120, 5120], P('tp')
Outputs:
- output 1: bfloat16 [1, 4096, 5120], P('dp', 'tp')
- output 2: bfloat16 [1, 4096, 40, 128], P('dp', None, 'tp')
- output 3: bfloat16 [1, 4096, 40, 128], P('dp', None, 'tp')
All inputs are finite; a program needn't handle non-finite values.
Results may differ from a plain program's by a relative error of at most 0.00944418.
Values are sent between devices in bfloat16 or wider.
A program may use at most 1 GiB of HBM per device.

v0:
```python
import jax
import jax.numpy as jnp
from jax import lax
from jax.sharding import PartitionSpec as P

HEAD_DIM = 128


def rope_tables(seq_len, head_dim):
    half_dim = head_dim // 2
    inv_freq = 10000.0 ** (-jnp.arange(half_dim, dtype=jnp.float32) * (2.0 / head_dim))
    angles = jnp.arange(seq_len, dtype=jnp.float32)[:, None] * inv_freq[None, :]
    return jnp.cos(angles), jnp.sin(angles)


def apply_rope(heads_in, cos_tab, sin_tab):
    half_dim = heads_in.shape[-1] // 2
    lower_half = heads_in[..., :half_dim]
    upper_half = heads_in[..., half_dim:]
    cos_bcast = cos_tab[None, :, None, :]
    sin_bcast = sin_tab[None, :, None, :]
    return jnp.concatenate([lower_half * cos_bcast - upper_half * sin_bcast, upper_half * cos_bcast + lower_half * sin_bcast], axis=-1)


def causal_attention(q_rot, k_rot, v_heads):
    seq_len = q_rot.shape[1]
    q_tile = min(seq_len, 128)
    score_scale = q_rot.shape[-1] ** -0.5
    tile_outs = []
    for tile_idx in range(seq_len // q_tile):
        q_start = tile_idx * q_tile
        q_stop = q_start + q_tile
        q_part = q_rot[:, q_start:q_stop]
        if tile_outs:
            q_part, prev_out = lax.optimization_barrier((q_part, tile_outs[-1]))
            tile_outs[-1] = prev_out
        scores = jnp.einsum('bqhd,bkhd->bhqk', q_part, k_rot[:, :q_stop], preferred_element_type=jnp.float32) * score_scale
        q_pos = q_start + jnp.arange(q_tile)
        k_pos = jnp.arange(q_stop)
        scores = jnp.where(q_pos[:, None] >= k_pos[None, :], scores, -1e30)
        prob_bf = jax.nn.softmax(scores, axis=-1).astype(jnp.bfloat16)
        tile_out = jnp.einsum('bhqk,bkhd->bqhd', prob_bf, v_heads[:, :q_stop], preferred_element_type=jnp.float32)
        tile_outs.append(tile_out.astype(jnp.bfloat16))
    return jnp.concatenate(tile_outs, axis=1)


def solution(mesh):
    def local_block(x_local, attn_gain, wq_cols, wk_cols, wv_cols, qg_cols, kg_cols, wo_rows):
        n_batch = x_local.shape[0]
        width = x_local.shape[2]
        x_f32 = x_local.astype(jnp.float32)
        inv_rms = lax.rsqrt(jnp.mean(x_f32 * x_f32, axis=-1, keepdims=True) + 1e-5)
        normed = (x_f32 * inv_rms * attn_gain).astype(jnp.bfloat16)
        h_full = lax.all_gather(normed, 'tp', axis=1, tiled=True)
        seq_len = h_full.shape[1]
        local_cols = wq_cols.shape[1]
        local_heads = local_cols // HEAD_DIM
        q_raw = jnp.einsum('btd,dc->btc', h_full, wq_cols, preferred_element_type=jnp.float32).astype(jnp.bfloat16)
        k_raw = jnp.einsum('btd,dc->btc', h_full, wk_cols, preferred_element_type=jnp.float32).astype(jnp.bfloat16)
        v_raw = jnp.einsum('btd,dc->btc', h_full, wv_cols, preferred_element_type=jnp.float32).astype(jnp.bfloat16)
        part_sq = jnp.stack([jnp.einsum('btc,btc->bt', q_raw, q_raw, preferred_element_type=jnp.float32), jnp.einsum('btc,btc->bt', k_raw, k_raw, preferred_element_type=jnp.float32)])
        total_sq = lax.psum(part_sq, 'tp')
        inv_norm = lax.rsqrt(total_sq / width + 1e-5)
        q_normed = q_raw.astype(jnp.float32) * inv_norm[0][..., None] * qg_cols
        k_normed = k_raw.astype(jnp.float32) * inv_norm[1][..., None] * kg_cols
        cos_tab, sin_tab = rope_tables(seq_len, HEAD_DIM)
        head_shape = (n_batch, seq_len, local_heads, HEAD_DIM)
        q_rot = apply_rope(q_normed.reshape(head_shape), cos_tab, sin_tab).astype(jnp.bfloat16)
        k_rot = apply_rope(k_normed.reshape(head_shape), cos_tab, sin_tab).astype(jnp.bfloat16)
        v_heads = v_raw.reshape(head_shape)
        attn_out = causal_attention(q_rot, k_rot, v_heads).reshape(n_batch, seq_len, local_cols)
        y_part = jnp.einsum('btc,cd->btd', attn_out, wo_rows, preferred_element_type=jnp.float32).astype(jnp.bfloat16)
        y_local = lax.psum_scatter(y_part, 'tp', scatter_dimension=1, tiled=True)
        hidden_out = (x_f32 + y_local.astype(jnp.float32)).astype(jnp.bfloat16)
        return (hidden_out, k_rot, v_heads)

    seq_spec = P('dp', 'tp', None)
    head_spec = P('dp', None, 'tp', None)
    col_spec = P(None, 'tp')
    return jax.shard_map(local_block, mesh=mesh, in_specs=(seq_spec, P(None), col_spec, col_spec, col_spec, P('tp'), P('tp'), P('tp', None)), out_specs=(seq_spec, head_spec, head_spec), check_vma=False)
```

profile of v0, /device:TPU:0, one launch (start us, length us, event | category | flops | bytes accessed | tf_op | source)
XLA Modules:
  0.0 1238.0 jit_solution(13222532890760630810)
XLA Ops:
  46.2 9.2 fusion.217
  55.5 155.4 %all-gather.2.cloned.1.call-done = bf16[1,4096,5120]{2,1,0:T(8,128)(2,1)} async-done(((bf16[1,512,5120]{2,1,0:T(8,128)(2,1)}), bf16[1,4096,5120]{2,1,0:T(8,128)(2,1)}) %all-gather.2.cloned.1.call-update) | async-done | bytes 41943056 | tf_op jit(solution)/shard_map/all_gather | solution.py:54
  210.9 34.2 %fusion.40 = (f32[4096]{0:T(1024)S(1)}, bf16[4096,640]{0,1:T(8,128)(2,1)}) fusion(bf16[5120,640]{1,0:T(8,128)(2,1)} %param.11, bf16[1,4096,5120]{2,1,0:T(8,128)(2,1)} %all-gather.2.cloned.1.call-done), kind=kOutput, calls=%fused_computation.48 | convolution fusion | flops 26854027264 | bytes 53755904 | tf_op jit(solution)/shard_map/btd,dc->btc/dot_general | solution.py:59
  245.1 34.2 %fusion.39 = (f32[4096]{0:T(1024)S(1)}, bf16[4096,640]{0,1:T(8,128)(2,1)}) fusion(bf16[5120,640]{1,0:T(8,128)(2,1)} %param.10, bf16[1,4096,5120]{2,1,0:T(8,128)(2,1)} %all-gather.2.cloned.1.call-done), kind=kOutput, calls=%fused_computation.47 | convolution fusion | flops 26854027264 | bytes 53755904 | tf_op jit(solution)/shard_map/btd,dc->btc/dot_general | solution.py:58
  279.3 22.6 %psum.7 = f32[2,1,4096]{2,1,0:T(1,128)S(1)} all-reduce(f32[2,1,4096]{2,1,0:T(1,128)S(1)} %pad_maximum_fusion.1), channel_id=1, replica_groups=mesh['dp'=1,'tp'=8] {'tp'}, use_global_device_ids=true, to_apply=%region_1.0 | all-reduce | flops 8192 | bytes 65536 | tf_op jit(solution)/shard_map/psum | solution.py:62
  320.0 8.4 copy.41
  328.4 8.4 copy.39
  336.8 8.4 copy.40
  345.2 8.4 copy.38
  353.6 22.3 %subtract_convert_fusion = (bf16[1,4096,5,64]{3,1,2,0:T(8,128)(2,1)S(1)}, bf16[1,4096,5,64]{3,1,2,0:T(8,128)(2,1)}, bf16[1,4096,5,64]{3,1,2,0:T(8,128)(2,1)}, bf16[1,4096,5,64]{3,1,2,0:T(8,128)(2,1)}) fusion(f32[1,4096,5,64]{3,1,2,0:T(8,128)} %copy.41, f32[1,4096,5,64]{3,1,2,0:T(8,128)} %copy.40, f32[4096,64]{1,0:T(8,128)} %get-tuple-element.176, ...), kind=kLoop, calls=%fused_computation.58 | loop fusion | flops 20971520 | bytes 33554432 | tf_op jit(solution)/shard_map/convert.4
  384.4 34.4 %fusion.60 = bf16[4096,640]{0,1:T(8,128)(2,1)} fusion(bf16[5120,640]{1,0:T(8,128)(2,1)} %param.12, bf16[1,4096,5120]{2,1,0:T(8,128)(2,1)} %all-gather.2.cloned.1.call-done), kind=kOutput, calls=%fused_computation.107 | convolution fusion | flops 26846167040 | bytes 53739520 | tf_op jit(solution)/shard_map/btd,dc->btc/dot_general | solution.py:60
  745.8 8.1 fusion.301
  764.7 8.8 fusion.300
  784.8 8.6 fusion.299
  805.1 8.8 fusion.298
  825.9 9.0 fusion.297
  847.1 9.3 fusion.296
  868.9 9.5 fusion.295
  891.9 9.9 fusion.294
  922.3 14.1 %fusion.722 = (f32[5,128]{1,0:T(8,128)S(1)}, f32[5,128,4096]{2,1,0:T(8,128)}) fusion(pred[128,4096]{1,0:T(8,128)(4,1)S(1)} %copy-done.50, bf16[4096,5,64]{2,0,1:T(8,128)(2,1)} %bitcast.739, bf16[4096,5,64]{2,0,1:T(8,128)(2,1)} %bitcast.738, bf16[1,128,5,128]{3,1,2,0:T(8,128)(2,1)S(1)} %copy-done.101), kind=kOutput, calls=%fused_computation.875 | convolution fusion | flops 692064256 | bytes 16419328 | tf_op jit(solution)/shard_map/sub | solution.py:41
  944.3 40.8 %convolution_convert_fusion = bf16[4096,5120]{1,0:T(8,128)(2,1)} fusion(bf16[4096,640]{0,1:T(8,128)(2,1)} %bitcast.789, bf16[640,5120]{1,0:T(8,128)(2,1)} %param.15), kind=kOutput, calls=%fused_computation.38 | convolution fusion | flops 26864517120 | bytes 53739520 | tf_op jit(solution)/shard_map/btc,cd->btd/dot_general | solution.py:72
  993.1 9.3 pad_maximum_fusion.2
  1002.4 220.3 %reduce-scatter.4.cloned.1.call-done = bf16[1,16,163840]{2,1,0:T(8,128)(2,1)} async-done(((bf16[1,128,163840]{2,1,0:T(8,128)(2,1)}), bf16[1,16,163840]{2,1,0:T(8,128)(2,1)}) %reduce-scatter.4.cloned.1.call-update) | async-done | bytes 5242896
  1222.7 8.3 fusion.45
  (431 shorter events, 511.9 us)
Async XLA Ops:
  7.2 203.8 %all-gather.2.cloned.1.call-start = ((), (), s32[]{:S(2)}) async-start(), calls=%async_computation.1 | async-start | bytes 47185920 | tf_op jit(solution)/shard_map/all_gather | solution.py:54
  16.4 1206.3 %reduce-scatter.4.cloned.1.call-start = ((), (), s32[]{:S(2)}) async-start(), calls=%async_computation.2 | async-start | bytes 47185920
  245.1 56.9 %copy-start.103 = (f32[640]{0:T(1024)S(1)}, f32[640]{0:T(1024)}, u32[]{:S(2)}) copy-start(f32[640]{0:T(1024)} %param.13) | copy-start | bytes 7684
  384.4 36.3 %copy-start.66 = (pred[128,256]{1,0:T(8,128)(4,1)S(1)}, pred[128,256]{1,0:T(8,128)(4,1)}, u32[]{:S(2)}) copy-start(pred[128,256]{1,0:T(8,128)(4,1)} %iota_compare_fusion.30) | copy-start | bytes 98308
  441.8 56.2 %copy-start.20 = (bf16[1,128,5,128]{3,1,2,0:T(8,128)(2,1)}, bf16[1,128,5,128]{3,1,2,0:T(8,128)(2,1)S(1)}, u32[]{:S(2)}) copy-start(bf16[1,128,5,128]{3,1,2,0:T(8,128)(2,1)S(1)} %get-tuple-element.82) | copy-start | bytes 491524
  891.8 14.9 %copy-start.78 = (bf16[1,128,5,128]{1,3,2,0:T(8,128)(2,1)S(1)}, bf16[1,128,5,128]{1,3,2,0:T(8,128)(2,1)}, u32[]{:S(2)}) copy-start(bf16[1,128,5,128]{1,3,2,0:T(8,128)(2,1)} %fusion.314) | copy-start | bytes 491524
  891.8 15.5 %copy-start.79 = (bf16[1,128,5,128]{1,3,2,0:T(8,128)(2,1)S(1)}, bf16[1,128,5,128]{1,3,2,0:T(8,128)(2,1)}, u32[]{:S(2)}) copy-start(bf16[1,128,5,128]{1,3,2,0:T(8,128)(2,1)} %fusion.289) | copy-start | bytes 491524
  891.8 16.2 %copy-start.80 = (bf16[1,128,5,128]{1,3,2,0:T(8,128)(2,1)S(1)}, bf16[1,128,5,128]{1,3,2,0:T(8,128)(2,1)}, u32[]{:S(2)}) copy-start(bf16[1,128,5,128]{1,3,2,0:T(8,128)(2,1)} %fusion.313) | copy-start | bytes 491524
  891.8 16.9 %copy-start.81 = (bf16[1,128,5,128]{1,3,2,0:T(8,128)(2,1)S(1)}, bf16[1,128,5,128]{1,3,2,0:T(8,128)(2,1)}, u32[]{:S(2)}) copy-start(bf16[1,128,5,128]{1,3,2,0:T(8,128)(2,1)} %fusion.312) | copy-start | bytes 491524
  891.8 17.5 %copy-start.82 = (bf16[1,128,5,128]{1,3,2,0:T(8,128)(2,1)S(1)}, bf16[1,128,5,128]{1,3,2,0:T(8,128)(2,1)}, u32[]{:S(2)}) copy-start(bf16[1,128,5,128]{1,3,2,0:T(8,128)(2,1)} %fusion.311) | copy-start | bytes 491524
  891.9 18.2 %copy-start.83 = (bf16[1,128,5,128]{1,3,2,0:T(8,128)(2,1)S(1)}, bf16[1,128,5,128]{1,3,2,0:T(8,128)(2,1)}, u32[]{:S(2)}) copy-start(bf16[1,128,5,128]{1,3,2,0:T(8,128)(2,1)} %fusion.288) | copy-start | bytes 491524
  891.9 18.9 %copy-start.84 = (bf16[1,128,5,128]{1,3,2,0:T(8,128)(2,1)S(1)}, bf16[1,128,5,128]{1,3,2,0:T(8,128)(2,1)}, u32[]{:S(2)}) copy-start(bf16[1,128,5,128]{1,3,2,0:T(8,128)(2,1)} %fusion.310) | copy-start | bytes 491524
  891.9 19.5 %copy-start.85 = (bf16[1,128,5,128]{1,3,2,0:T(8,128)(2,1)S(1)}, bf16[1,128,5,128]{1,3,2,0:T(8,128)(2,1)}, u32[]{:S(2)}) copy-start(bf16[1,128,5,128]{1,3,2,0:T(8,128)(2,1)} %fusion.309) | copy-start | bytes 491524
  891.9 20.2 %copy-start.87 = (bf16[1,128,5,128]{1,3,2,0:T(8,128)(2,1)S(1)}, bf16[1,128,5,128]{1,3,2,0:T(8,128)(2,1)}, u32[]{:S(2)}) copy-start(bf16[1,128,5,128]{1,3,2,0:T(8,128)(2,1)} %fusion.308) | copy-start | bytes 491524
  901.8 14.4 %copy-start.93 = (bf16[1,128,5,128]{1,3,2,0:T(8,128)(2,1)S(1)}, bf16[1,128,5,128]{1,3,2,0:T(8,128)(2,1)}, u32[]{:S(2)}) copy-start(bf16[1,128,5,128]{1,3,2,0:T(8,128)(2,1)} %fusion.302) | copy-start | bytes 491524
  901.8 15.1 %copy-start.94 = (bf16[1,128,5,128]{1,3,2,0:T(8,128)(2,1)S(1)}, bf16[1,128,5,128]{1,3,2,0:T(8,128)(2,1)}, u32[]{:S(2)}) copy-start(bf16[1,128,5,128]{1,3,2,0:T(8,128)(2,1)} %fusion.301) | copy-start | bytes 491524
  901.8 16.4 %copy-start.95 = (bf16[1,128,5,128]{1,3,2,0:T(8,128)(2,1)S(1)}, bf16[1,128,5,128]{1,3,2,0:T(8,128)(2,1)}, u32[]{:S(2)}) copy-start(bf16[1,128,5,128]{1,3,2,0:T(8,128)(2,1)} %fusion.299) | copy-start | bytes 491524
  901.8 17.1 %copy-start.96 = (bf16[1,128,5,128]{1,3,2,0:T(8,128)(2,1)S(1)}, bf16[1,128,5,128]{1,3,2,0:T(8,128)(2,1)}, u32[]{:S(2)}) copy-start(bf16[1,128,5,128]{1,3,2,0:T(8,128)(2,1)} %fusion.298) | copy-start | bytes 491524
  901.8 17.7 %copy-start.97 = (bf16[1,128,5,128]{1,3,2,0:T(8,128)(2,1)S(1)}, bf16[1,128,5,128]{1,3,2,0:T(8,128)(2,1)}, u32[]{:S(2)}) copy-start(bf16[1,128,5,128]{1,3,2,0:T(8,128)(2,1)} %fusion.297) | copy-start | bytes 491524
  901.8 18.4 %copy-start.98 = (bf16[1,128,5,128]{1,3,2,0:T(8,128)(2,1)S(1)}, bf16[1,128,5,128]{1,3,2,0:T(8,128)(2,1)}, u32[]{:S(2)}) copy-start(bf16[1,128,5,128]{1,3,2,0:T(8,128)(2,1)} %fusion.296) | copy-start | bytes 491524
  901.9 19.1 %copy-start.99 = (bf16[1,128,5,128]{1,3,2,0:T(8,128)(2,1)S(1)}, bf16[1,128,5,128]{1,3,2,0:T(8,128)(2,1)}, u32[]{:S(2)}) copy-start(bf16[1,128,5,128]{1,3,2,0:T(8,128)(2,1)} %fusion.295) | copy-start | bytes 491524
  901.9 19.8 %copy-start.100 = (bf16[1,128,5,128]{1,3,2,0:T(8,128)(2,1)S(1)}, bf16[1,128,5,128]{1,3,2,0:T(8,128)(2,1)}, u32[]{:S(2)}) copy-start(bf16[1,128,5,128]{1,3,2,0:T(8,128)(2,1)} %fusion.294) | copy-start | bytes 491524
  901.9 20.4 %copy-start.50 = (pred[128,4096]{1,0:T(8,128)(4,1)S(1)}, pred[128,4096]{1,0:T(8,128)(4,1)}, u32[]{:S(2)}) copy-start(pred[128,4096]{1,0:T(8,128)(4,1)} %iota_compare_fusion) | copy-start | bytes 1572868
  902.6 19.7 %copy-start.101 = (bf16[1,128,5,128]{3,1,2,0:T(8,128)(2,1)S(1)}, bf16[1,128,5,128]{3,1,2,0:T(8,128)(2,1)}, u32[]{:S(2)}) copy-start(bf16[1,128,5,128]{3,1,2,0:T(8,128)(2,1)} %pad_maximum_fusion) | copy-start | bytes 491524
  (91 other events, 598.7 us)
Sparse Core Ops, SparseCore 0:
  16.5 194.3 all-gather.1
  985.2 237.4 reduce-scatter.3
where the time goes:
time: 1250 us; the launch traced here: 1240 us
  matrix products  564 us (45%)
  waiting for transfers between devices  376 us (30%)
  other arithmetic  142 us (11%)
  local copies, waits for them, and re-layouts  118 us (9%)
  blocking collectives  22.6 us (2%)
  between operations  15.5 us (1%)
    unnamed x3, waiting for transfers between devices  220 us
    dot_general x32, matrix products, causal_attention(): jnp.einsum('bhqk,bkhd->bqhd', prob_bf, v_heads[:, :q_stop], preferred_ele...  197 us
    all_gather x1, waiting for transfers between devices, local_block(): h_full = lax.all_gather(normed, 'tp', axis=1, tiled=True)  155 us
    dot_general x31, matrix products, causal_attention(): jnp.einsum('bqhd,bkhd->bhqk', q_part, k_rot[:, :q_stop], preferred_elemen...  142 us
    unnamed x262, local copies, waits for them, and re-layouts  109 us
    sub x18, matrix products, causal_attention(): prob_bf = jax.nn.softmax(scores, axis=-1).astype(jnp.bfloat16)  82 us
    dot_general x1, matrix products, local_block(): jnp.einsum('btc,cd->btd', attn_out, wo_rows, preferred_element_type=jnp.f...  40.8 us
    dot_general x1, matrix products, local_block(): jnp.einsum('btd,dc->btc', h_full, wv_cols, preferred_element_type=jnp.flo...  34.4 us
  transfers between devices with their start and end apart: 2, of which 2 were waited for; matrix products, arithmetic and copies ran while one was open for 5% of the time, Pallas kernels for 0%

commit v1 on v0

v1 whole, which is shorter than its diff:
```python
import functools

import jax
import jax.numpy as jnp
import numpy as np
from jax import lax
from jax.experimental import pallas as pl
from jax.experimental.pallas import tpu as pltpu
from jax.sharding import PartitionSpec as P

MESH = pl.DeviceIdType.MESH
HEAD_DIM = 128
HEADS = 5
COLS = HEADS * HEAD_DIM
WIDTH = 5120
BLOCK = 512
TP = 8
SEQ = TP * BLOCK
PIECES = 4
PIECE = BLOCK // PIECES
UNIT = 256
STEPS = 8
ROWS = BLOCK // STEPS
HALF = WIDTH // 2
TILE = 512
F32 = jnp.float32
BF16 = jnp.bfloat16
SIB, XN, YN, DG, SX, SY, SDG = range(7)


class Place:
    def __init__(self):
        me = lax.axis_index("tp")
        self.dp = lax.axis_index("dp")
        self.me = me
        self.core = me % 2
        self.x = (me // 2) % 2
        self.y = me // 4

    def at(self, fx, fy, fc):
        x = self.x + fx * (1 - 2 * self.x)
        y = self.y + fy * (1 - 2 * self.y)
        c = self.core + fc * (1 - 2 * self.core)
        return (y * 2 + x) * 2 + c

    def kind(self, k):
        fx, fy, fc = ((0, 0, 1), (1, 0, 0), (0, 1, 0), (1, 1, 0), (1, 0, 1), (0, 1, 1), (1, 1, 1))[k]
        return self.at(fx, fy, fc)

    def dev(self, index):
        return (self.dp, index)


def barrier_with(place, kinds):
    sem = pltpu.get_barrier_semaphore()
    for k in kinds:
        pl.semaphore_signal(sem, inc=1, device_id=place.dev(place.kind(k)), device_id_type=MESH)
    pl.semaphore_wait(sem, len(kinds))


def diagonal():
    r = lax.broadcasted_iota(jnp.int32, (128, 128), 0)
    c = lax.broadcasted_iota(jnp.int32, (128, 128), 1)
    return r == c


def gather_project(h_ref, wq_ref, wk_ref, wv_ref, qkv_ref, ssq_ref, hbuf,
                   w_v, h_v, st, ssq_v, w_sem, h_sem, o_sem, send_sem, recv_sem, ss_send, ss_recv, ss_loc):
    place = Place()
    for n, w in enumerate((wq_ref, wk_ref, wv_ref)):
        pltpu.make_async_copy(w, w_v.at[n], w_sem.at[n]).start()
    barrier_with(place, range(7))

    def copy(src_ref, block, p, send, kind, target):
        return pltpu.make_async_remote_copy(
            src_ref=src_ref, dst_ref=hbuf.at[block, pl.ds(p * PIECE, PIECE)],
            send_sem=send_sem.at[send, p], recv_sem=recv_sem.at[kind, p],
            device_id=place.dev(place.kind(target)), device_id_type=MESH)

    def own(p, send, kind):
        return copy(h_ref.at[pl.ds(p * PIECE, PIECE)], place.me, p, send, kind, kind)

    def relay(owner, p, send, kind, target):
        block = place.kind(owner)
        return copy(hbuf.at[block, pl.ds(p * PIECE, PIECE)], block, p, send, kind, target)

    def arrived(kind, p):
        relay(kind, p, 0, kind, SIB).wait_recv()

    for p in range(PIECES):
        own(p, 0, XN).start()
        own(p, 1, YN).start()
        own(p, 2, SIB).start()

    def forwards(p):
        out = [(XN, p, 3, SX, SIB), (YN, p, 4, SY, SIB)]
        out.append((XN, p, 5, DG, YN) if p % 2 == 0 else (YN, p, 5, DG, XN))
        return out

    def unit(u):
        a = u // 4
        v = u - 4
        w = v % 4
        z = u - 12
        near = a == 0
        far = a == 3
        fc = jnp.where(near, u // 2, jnp.where(far, z % 2, w // 2))
        half = jnp.where(near, u % 2, jnp.where(far, z // 2, v // 4))
        fy = jnp.where(near, 0, jnp.where(far, 1, w % 2))
        fx = jnp.where(near, 0, jnp.where(far, 1, 1 - w % 2))
        return place.at(fx, fy, fc), half

    def load(u, slot, own_rows):
        block, half = unit(u)
        rows = pl.ds(pl.multiple_of(half * UNIT, UNIT), UNIT)
        if own_rows:
            return pltpu.make_async_copy(h_ref.at[rows], h_v.at[slot], h_sem.at[slot])
        return pltpu.make_async_copy(hbuf.at[block, rows], h_v.at[slot], h_sem.at[slot])

    def start_load(u):
        @pl.when(u < 2)
        def _():
            load(u, u % 2, True).start()

        @pl.when(u >= 2)
        def _():
            load(u, u % 2, False).start()

    def store(u, slot):
        block, half = unit(u)
        rows = pl.ds(pl.multiple_of(block * BLOCK + half * UNIT, UNIT), UNIT)
        return pltpu.make_async_copy(st.at[slot], qkv_ref.at[:, :, rows, :], o_sem.at[slot])

    eye = diagonal()

    def step(u, carry):
        slot = u % 2
        for first, p0 in ((4, 0), (8, 2)):
            @pl.when(u == first)
            def _(p0=p0):
                for p in (p0, p0 + 1):
                    arrived(XN, p)
                    arrived(YN, p)
                    for f in forwards(p):
                        relay(*f).start()
        for first, p0 in ((12, 0), (14, 2)):
            @pl.when(u == first)
            def _(p0=p0):
                for p in (p0, p0 + 1):
                    arrived(DG, p)
                    relay(DG, p, 6, SDG, SIB).start()

        @pl.when((u % 4 == 0) | (u == 14))
        def _():
            start_load(u)

        for nxt, kind, p0 in ((2, SIB, 0), (3, SIB, 2), (6, SX, 0), (7, SY, 0), (10, SX, 2), (11, SY, 2), (13, SDG, 0), (15, SDG, 2)):
            @pl.when(u + 1 == nxt)
            def _(kind=kind, p0=p0):
                arrived(kind, p0)
                arrived(kind, p0 + 1)

        @pl.when(((u + 1) % 4 != 0) & (u + 1 != 14))
        def _():
            start_load(u + 1)

        @pl.when(u == 0)
        def _():
            for n, w in enumerate((wq_ref, wk_ref, wv_ref)):
                pltpu.make_async_copy(w, w_v.at[n], w_sem.at[n]).wait()

        load(u, slot, False).wait()

        @pl.when(u >= 2)
        def _():
            store(u - 2, slot).wait()

        block, half = unit(u)

        def part(n, c):
            r = jnp.dot(h_v[slot], w_v[n], preferred_element_type=F32).astype(BF16)
            for h in range(HEADS):
                st[slot, n, h] = r[:, h * HEAD_DIM:(h + 1) * HEAD_DIM]

            @pl.when(n < 2)
            def _():
                rf = r.astype(F32)
                col = jnp.sum(rf * rf, axis=1, keepdims=True)
                for b in range(UNIT // 128):
                    row = jnp.sum(jnp.where(eye, col[b * 128:(b + 1) * 128], 0.0), axis=0, keepdims=True)
                    ssq_v[pl.ds(block * 8 + n * 4 + half * 2 + b, 1), :] = row
            return c

        lax.fori_loop(0, 3, part, 0)
        store(u, slot).start()
        return carry

    lax.fori_loop(0, 16, step, 0)

    def share(k):
        return pltpu.make_async_remote_copy(
            src_ref=ssq_v, dst_ref=ssq_ref.at[place.me], send_sem=ss_send.at[k], recv_sem=ss_recv.at[k],
            device_id=place.dev(place.kind(k)), device_id_type=MESH)

    def shared(k):
        return pltpu.make_async_remote_copy(
            src_ref=ssq_v, dst_ref=ssq_ref.at[place.kind(k)], send_sem=ss_send.at[k], recv_sem=ss_recv.at[k],
            device_id=place.dev(place.kind(k)), device_id_type=MESH)

    for k in range(7):
        share(k).start()
    mine = pltpu.make_async_copy(ssq_v, ssq_ref.at[place.me], ss_loc)
    mine.start()
    store(14, 0).wait()
    store(15, 1).wait()
    for p in range(PIECES):
        own(p, 0, XN).wait_send()
        own(p, 1, YN).wait_send()
        own(p, 2, SIB).wait_send()
        for f in forwards(p):
            relay(*f).wait_send()
        relay(DG, p, 6, SDG, SIB).wait_send()
    mine.wait()
    for k in range(7):
        share(k).wait_send()
        shared(k).wait_recv()


def gather_project_call(h, wq, wk, wv):
    any_spec = pl.BlockSpec(memory_space=pl.ANY)
    return pl.pallas_call(
        gather_project,
        out_shape=[jax.ShapeDtypeStruct((3, HEADS, SEQ, HEAD_DIM), BF16),
                   jax.ShapeDtypeStruct((TP, 64, 128), F32),
                   jax.ShapeDtypeStruct((TP, BLOCK, WIDTH), BF16)],
        in_specs=[any_spec] * 4,
        out_specs=[any_spec] * 3,
        scratch_shapes=[
            pltpu.VMEM((3, WIDTH, COLS), BF16),
            pltpu.VMEM((2, UNIT, WIDTH), BF16),
            pltpu.VMEM((2, 3, HEADS, UNIT, HEAD_DIM), BF16),
            pltpu.VMEM((64, 128), F32),
            pltpu.SemaphoreType.DMA((3,)),
            pltpu.SemaphoreType.DMA((2,)),
            pltpu.SemaphoreType.DMA((2,)),
            pltpu.SemaphoreType.DMA((7, PIECES)),
            pltpu.SemaphoreType.DMA((7, PIECES)),
            pltpu.SemaphoreType.DMA((7,)),
            pltpu.SemaphoreType.DMA((7,)),
            pltpu.SemaphoreType.DMA(()),
        ],
        compiler_params=pltpu.CompilerParams(collective_id=0, has_side_effects=True, vmem_limit_bytes=60 * 2**20),
        name="gather_project",
    )(h, wq, wk, wv)


def rotate_heads(qk_ref, ssq_ref, gain_ref, tab_ref, q_ref, k_ref):
    eye = diagonal()
    total = jnp.sum(ssq_ref[...], axis=0)
    low = lax.broadcasted_iota(jnp.int32, (128, 128), 1) < 64
    for b in range(BLOCK // 128):
        rows = slice(b * 128, (b + 1) * 128)
        t = tab_ref[rows, :]
        turned = pltpu.roll(t, 64, 1)
        cos = jnp.where(low, t, turned)
        sin = jnp.where(low, -turned, t)
        for n in range(2):
            col = jnp.sum(jnp.where(eye, total[n * 4 + b:n * 4 + b + 1], 0.0), axis=1, keepdims=True)
            inv = lax.rsqrt(col / WIDTH + 1e-5)
            for h in range(HEADS):
                x = qk_ref[n, h, rows, :].astype(F32) * inv * gain_ref[n, h:h + 1, :]
                r = (x * cos + pltpu.roll(x, 64, 1) * sin).astype(BF16)
                if n == 0:
                    for g in range(128 // ROWS):
                        q_ref[h, b * (128 // ROWS) + g, 0] = r[g * ROWS:(g + 1) * ROWS]
                else:
                    k_ref[h, rows, :] = r


def rotate_heads_call(qkv, ssq, gains, table):
    return pl.pallas_call(
        rotate_heads,
        grid=(TP,),
        out_shape=[jax.ShapeDtypeStruct((HEADS, STEPS, TP, ROWS, HEAD_DIM), BF16),
                   jax.ShapeDtypeStruct((HEADS, SEQ, HEAD_DIM), BF16)],
        in_specs=[pl.BlockSpec((2, HEADS, BLOCK, HEAD_DIM), lambda i: (0, 0, i, 0)),
                  pl.BlockSpec((TP, 8, 128), lambda i: (0, i, 0)),
                  pl.BlockSpec((2, HEADS, HEAD_DIM), lambda i: (0, 0, 0)),
                  pl.BlockSpec((BLOCK, 128), lambda i: (i, 0))],
        out_specs=[pl.BlockSpec((HEADS, STEPS, 1, ROWS, HEAD_DIM), lambda i: (0, 0, i, 0, 0)),
                   pl.BlockSpec((HEADS, BLOCK, HEAD_DIM), lambda i: (0, i, 0))],
        name="rotate_heads",
    )(qkv, ssq, gains, table)


def attend_scatter(q_ref, k_ref, qkv_ref, wo_ref, x_ref, out_ref,
                   q_v, k_v, v_v, wo_v, o_v, ysend, recv0, s1, r1, keep, fin, s2, r2, x_v, ost,
                   ld_sem, wo_sem, x_sem, out_sem, y_send, y_recv, s1_send, s1_recv, s2_send, s2_recv):
    place = Place()
    scale = float(HEAD_DIM ** -0.5 * np.log2(np.e))

    def loads(h):
        return (pltpu.make_async_copy(q_ref.at[h], q_v.at[h], ld_sem.at[0, h]),
                pltpu.make_async_copy(k_ref.at[h], k_v.at[h], ld_sem.at[1, h]),
                pltpu.make_async_copy(qkv_ref.at[2, h], v_v.at[h], ld_sem.at[2, h]))

    for h in range(HEADS):
        for c in loads(h):
            c.start()
    pltpu.make_async_copy(wo_ref, wo_v, wo_sem).start()
    barrier_with(place, (SIB, XN, YN))

    def remote(src, dst, send, recv, kind):
        return pltpu.make_async_remote_copy(src_ref=src, dst_ref=dst, send_sem=send, recv_sem=recv,
                                            device_id=place.dev(place.kind(kind)), device_id_type=MESH)

    def to_sib(s):
        return remote(ysend, recv0.at[s % 2], y_send, y_recv.at[s % 2], SIB)

    def hop1(s, half):
        b = s % 2
        return remote(s1.at[b, half], r1.at[b, half], s1_send.at[b, half], s1_recv.at[b, half], (XN, YN)[half])

    def hop2(s, half):
        b = s % 2
        return remote(s2.at[b, half], r2.at[b, half], s2_send.at[b, half], s2_recv.at[b, half], (YN, XN)[half])

    def x_load(s):
        return pltpu.make_async_copy(x_ref.at[pl.ds(pl.multiple_of(s * ROWS, ROWS), ROWS)], x_v, x_sem)

    def out_store(s):
        return pltpu.make_async_copy(ost.at[s % 2], out_ref.at[pl.ds(pl.multiple_of(s * ROWS, ROWS), ROWS)], out_sem.at[s % 2])

    def gathered(b, half, other_core):
        c = place.core + other_core * (1 - 2 * place.core)
        order = ((0, 0), (0, 1), (1, 0), (1, 1)) if half == 0 else ((0, 0), (1, 0), (0, 1), (1, 1))
        parts = []
        for fx, fy in order:
            d = place.at(fx, fy, 0) // 2 * 2 + c
            parts.append(o_v[b, pl.ds(pl.multiple_of(d * ROWS, ROWS), ROWS), :])
        return jnp.concatenate(parts, axis=0)

    def tiles(body):
        def run(t, c):
            body(pl.ds(pl.multiple_of(t * TILE, TILE), TILE), t)
            return c
        lax.fori_loop(0, HALF // TILE, run, 0)

    def wo_tile(half, t):
        return wo_v[:, pl.ds(pl.multiple_of(half * HALF + t * TILE, TILE), TILE)]

    def project_sib(s):
        b = s % 2

        @pl.when(s >= 1)
        def _():
            to_sib(s - 1).wait_send()

        for half in range(2):
            rows = gathered(b, half, 1)

            def body(cols, t, half=half, rows=rows):
                ysend[half, :, cols] = jnp.dot(rows, wo_tile(half, t), preferred_element_type=F32).astype(BF16)
            tiles(body)
        to_sib(s).start()

    def stage1(s):
        b = s % 2
        to_sib(s).wait_recv()

        @pl.when(s >= 2)
        def _():
            for half in range(2):
                hop1(s - 2, half).wait_send()

        for half in range(2):
            rows = gathered(b, half, 0)

            def body(cols, t, half=half, rows=rows):
                y = jnp.dot(rows, wo_tile(half, t), preferred_element_type=F32) + recv0[b, half, :, cols].astype(F32)
                keep[half, :, cols] = y[:128]
                s1[b, half, :, cols] = y[128:].astype(BF16)
            tiles(body)
            hop1(s, half).start()

    def stage2(s):
        b = s % 2

        @pl.when(s >= 2)
        def _():
            for half in range(2):
                hop2(s - 2, half).wait_send()

        for half in range(2):
            hop1(s, half).wait_recv()

            def body(cols, t, half=half):
                y = keep[half, :, cols] + r1[b, half, :, cols].astype(F32)
                fin[half, :, cols] = y[:ROWS]
                s2[b, half, :, cols] = y[ROWS:].astype(BF16)
            tiles(body)
            hop2(s, half).start()

    def stage3(s):
        b = s % 2
        x_load(s).wait()

        @pl.when(s >= 2)
        def _():
            out_store(s - 2).wait()

        for half in range(2):
            hop2(s, half).wait_recv()

            def body(cols, t, half=half):
                y = (fin[half, :, cols] + r2[b, half, :, cols].astype(F32)).astype(BF16).astype(F32)
                whole = pl.ds(pl.multiple_of(half * HALF + t * TILE, TILE), TILE)
                ost[b, :, whole] = (x_v[:, whole].astype(F32) + y).astype(BF16)
            tiles(body)
        out_store(s).start()

    def attend(i, h):
        q = q_v[h, i]
        dims = (((1,), (1,)), ((), ()))

        def scores(j):
            return lax.dot_general(q[j * ROWS:], k_v[h, j * BLOCK:(j + 1) * BLOCK, :], dims, preferred_element_type=F32)

        row = lax.broadcasted_iota(jnp.int32, (ROWS, BLOCK), 0) + i * ROWS
        keep_mask = lax.broadcasted_iota(jnp.int32, (ROWS, BLOCK), 1) <= row
        m = l = acc = None
        ahead = scores(0)
        for j in range(TP):
            s = ahead
            if j + 1 < TP:
                ahead = scores(j + 1)
            top = jnp.where(keep_mask, s[:ROWS], -1e30)
            s = top if j == TP - 1 else jnp.concatenate([top, s[ROWS:]], axis=0)
            peak = jnp.max(s, axis=1, keepdims=True) * scale
            new_m = peak if j == 0 else jnp.maximum(m, peak)
            p = jnp.exp2(s * scale - new_m)
            part = p[:, 0:128]
            for c in range(1, BLOCK // 128):
                part = part + p[:, c * 128:(c + 1) * 128]
            pv = jnp.dot(p.astype(BF16), v_v[h, j * BLOCK:(j + 1) * BLOCK, :], preferred_element_type=F32)
            if j == 0:
                l, acc = part, pv
            else:
                alpha = jnp.exp2(m - new_m)
                l = l * alpha + part
                acc = acc * alpha + pv
            total = jnp.sum(l[:ROWS], axis=1, keepdims=True)
            o_v[i % 2, j * ROWS:(j + 1) * ROWS, pl.ds(pl.multiple_of(h * HEAD_DIM, HEAD_DIM), HEAD_DIM)] = (
                acc[:ROWS] / total).astype(BF16)
            if j + 1 < TP:
                m, l, acc = new_m[ROWS:], l[ROWS:], acc[ROWS:]

    def step(i, carry):
        @pl.when(i >= 3)
        def _():
            x_load(i - 3).start()

        def head(h, c):
            @pl.when(h == 1)
            def _():
                @pl.when(i >= 3)
                def _():
                    stage3(i - 3)

                @pl.when((i >= 2) & (i < STEPS + 2))
                def _():
                    stage2(i - 2)

                @pl.when((i >= 1) & (i < STEPS + 1))
                def _():
                    stage1(i - 1)

            @pl.when(i < STEPS)
            def _():
                @pl.when(i == 0)
                def _():
                    for cp in loads(h):
                        cp.wait()
                attend(i, h)
            return c

        lax.fori_loop(0, HEADS, head, 0)

        @pl.when(i < STEPS)
        def _():
            @pl.when(i == 0)
            def _():
                pltpu.make_async_copy(wo_ref, wo_v, wo_sem).wait()
            project_sib(i)
        return carry

    lax.fori_loop(0, STEPS + 3, step, 0)
    to_sib(STEPS - 1).wait_send()
    for s in (STEPS - 2, STEPS - 1):
        for half in range(2):
            hop1(s, half).wait_send()
            hop2(s, half).wait_send()
        out_store(s).wait()


def attend_scatter_call(q, k, qkv, wo, x):
    any_spec = pl.BlockSpec(memory_space=pl.ANY)
    return pl.pallas_call(
        attend_scatter,
        out_shape=jax.ShapeDtypeStruct((BLOCK, WIDTH), BF16),
        in_specs=[any_spec] * 5,
        out_specs=any_spec,
        scratch_shapes=[
            pltpu.VMEM((HEADS, STEPS, BLOCK, HEAD_DIM), BF16),
            pltpu.VMEM((HEADS, SEQ, HEAD_DIM), BF16),
            pltpu.VMEM((HEADS, SEQ, HEAD_DIM), BF16),
            pltpu.VMEM((COLS, WIDTH), BF16),
            pltpu.VMEM((2, BLOCK, COLS), BF16),
            pltpu.VMEM((2, 4 * ROWS, HALF), BF16),
            pltpu.VMEM((2, 2, 4 * ROWS, HALF), BF16),
            pltpu.VMEM((2, 2, 2 * ROWS, HALF), BF16),
            pltpu.VMEM((2, 2, 2 * ROWS, HALF), BF16),
            pltpu.VMEM((2, 2 * ROWS, HALF), F32),
            pltpu.VMEM((2, ROWS, HALF), F32),
            pltpu.VMEM((2, 2, ROWS, HALF), BF16),
            pltpu.VMEM((2, 2, ROWS, HALF), BF16),
            pltpu.VMEM((ROWS, WIDTH), BF16),
            pltpu.VMEM((2, ROWS, WIDTH), BF16),
            pltpu.SemaphoreType.DMA((3, HEADS)),
            pltpu.SemaphoreType.DMA(()),
            pltpu.SemaphoreType.DMA(()),
            pltpu.SemaphoreType.DMA((2,)),
            pltpu.SemaphoreType.DMA(()),
            pltpu.SemaphoreType.DMA((2,)),
            pltpu.SemaphoreType.DMA((2, 2)),
            pltpu.SemaphoreType.DMA((2, 2)),
            pltpu.SemaphoreType.DMA((2, 2)),
            pltpu.SemaphoreType.DMA((2, 2)),
        ],
        compiler_params=pltpu.CompilerParams(collective_id=1, has_side_effects=True, vmem_limit_bytes=62 * 2**20),
        name="attend_scatter",
    )(q, k, qkv, wo, x)


def rope_table():
    half = HEAD_DIM // 2
    freq = (10000.0 ** (-np.arange(half, dtype=np.float64) * (2.0 / HEAD_DIM))).astype(np.float32)
    angle = (np.arange(SEQ, dtype=np.float32)[:, None] * freq[None, :]).astype(np.float64)
    return np.concatenate([np.cos(angle), np.sin(angle)], axis=1).astype(np.float32)


def solution(mesh):
    table = rope_table()

    def local_block(x_local, attn_gain, wq, wk, wv, q_gain, k_gain, wo):
        x = x_local[0]
        xf = x.astype(F32)
        inv = lax.rsqrt(jnp.mean(xf * xf, axis=-1, keepdims=True) + 1e-5)
        h = (xf * inv * attn_gain).astype(BF16)
        qkv, ssq, _ = gather_project_call(h, wq, wk, wv)
        gains = jnp.stack([q_gain, k_gain]).reshape(2, HEADS, HEAD_DIM)
        q, k = rotate_heads_call(qkv, ssq, gains, jnp.asarray(table))
        q = q.reshape(HEADS, STEPS, BLOCK, HEAD_DIM)
        out = attend_scatter_call(q, k, qkv, wo, x)
        k_cache = jnp.transpose(k, (1, 0, 2))[None]
        v_cache = jnp.transpose(qkv[2], (1, 0, 2))[None]
        return out[None], k_cache, v_cache

    seq_spec = P("dp", "tp", None)
    head_spec = P("dp", None, "tp", None)
    col_spec = P(None, "tp")
    return jax.shard_map(local_block, mesh=mesh,
                         in_specs=(seq_spec, P(None), col_spec, col_spec, col_spec, P("tp"), P("tp"), P("tp", None)),
                         out_specs=(seq_spec, head_spec, head_spec), check_vma=False)
```

time: 1250 us -> 435 us (0.35)
  matrix products: 564 us -> 0 us
  Pallas kernels: 0 us -> 416 us
  waiting for transfers between devices: 376 us -> 0 us
  other arithmetic: 142 us -> 9.46 us
  local copies, waits for them, and re-layouts: 118 us -> 8 us
  blocking collectives: 22.6 us -> 0 us
  between operations: 15.5 us -> 0.69 us
    dot_general x67 -> x0, matrix products: 482 us -> none  [the longest x32 197 us: causal_attention(): jnp.einsum('bhqk,bkhd->bqhd', prob_bf, v_heads[:, :q_stop], preferred_ele...]
    pallas_call x0 -> x3, Pallas kernels: none -> 416 us  [the longest x1 201 us: attend_scatter_call(): pl.pallas_call(attend_scatter, out_shape=jax.ShapeDtypeStruct((BLOCK, WID...]
    unnamed x3 -> x0, waiting for transfers between devices: 220 us -> none
    all_gather x1 -> x0, waiting for transfers between devices: 155 us -> none  [local_block(): h_full = lax.all_gather(normed, 'tp', axis=1, tiled=True)]
    unnamed x262 -> x11, local copies, waits for them, and re-layouts: 109 us -> 2.66 us
    sub x18 -> x0, matrix products: 82 us -> none  [causal_attention(): prob_bf = jax.nn.softmax(scores, axis=-1).astype(jnp.bfloat16)]
    sub x14 -> x0, other arithmetic: 31.6 us -> none  [causal_attention(): prob_bf = jax.nn.softmax(scores, axis=-1).astype(jnp.bfloat16)]
    ge x32 -> x0, other arithmetic: 29.4 us -> none  [causal_attention(): scores = jnp.where(q_pos[:, None] >= k_pos[None, :], scores, -1e+30)]
  transfers between devices with their start and end apart: 2 -> 0, of which waited for: 2 -> 0; matrix products, arithmetic and copies ran while one was open for 5% -> 0% of each run, Pallas kernels for 0% -> 0%
where the time goes in v1:
time: 435 us
  Pallas kernels  416 us (96%)
  other arithmetic  9.46 us (2%)
  local copies, waits for them, and re-layouts  8 us (2%)
    pallas_call x1, Pallas kernels, attend_scatter_call(): pl.pallas_call(attend_scatter, out_shape=jax.ShapeDtypeStruct((BLOCK, WID...  201 us
    pallas_call x1, Pallas kernels, gather_project_call(): pl.pallas_call(gather_project, out_shape=[jax.ShapeDtypeStruct((3, HEADS,...  199 us
    pallas_call x1, Pallas kernels, rotate_heads_call(): pl.pallas_call(rotate_heads, grid=(TP,), out_shape=[jax.ShapeDtypeStruct(...  16.2 us

profile of v1, /device:TPU:0, one launch (start us, length us, event | category | flops | bytes accessed | tf_op | source)
XLA Modules:
  0.0 434.5 jit_solution(16574997250112093853)
XLA Ops:
  0.6 0.0 copy-start
  0.6 3.7 fusion
  4.4 0.3 copy-done
  4.7 5.1 %fusion.2.h_ref = bf16[512,5120]{1,0:T(8,128)(2,1)} fusion(f32[5120]{0:T(1024)} %param.10, f32[512]{0:T(512)S(1)} %add_rsqrt_fusion, bf16[1,512,5120]{2,1,0:T(8,128)(2,1)S(1)} %copy-done), kind=kLoop, calls=%fused_computation.4 | loop fusion | flops 10485760 | bytes 10508288 | tf_op jit(solution)/shard_map/convert_element_type | solution.py:559
  9.8 0.0 copy-start.1
  9.8 0.0 copy-start.2
  9.8 198.8 %gather_project.1 = (bf16[3,5,4096,128]{3,2,1,0:T(8,128)(2,1)}, f32[8,64,128]{2,1,0:T(8,128)}, bf16[8,512,5120]{2,1,0:T(8,128)(2,1)}) custom-call(bf16[512,5120]{1,0:T(8,128)(2,1)} %fusion.2.h_ref, bf16[5120,640]{1,0:T(8,128)(2,1)} %wq_ref.1, bf16[5120,640]{1,0:T(8,128)(2,1)} %wk_ref.1, bf16[5120,640]{1,0:T(8,128)(2,1)} %wv_ref.1), custom_call_target="tpu_custom_call" | custom-call | tf_op jit(solution)/shard_map/gather_project/pallas_call | solution.py:231
  208.6 0.0 copy-done.1
  208.7 0.0 copy-done.2
  208.7 0.6 pad_maximum_fusion.gain_ref
  209.3 16.2 %rotate_heads.1 = (bf16[5,8,8,64,128]{4,3,2,1,0:T(8,128)(2,1)}, bf16[5,4096,128]{2,1,0:T(8,128)(2,1)}) custom-call(bf16[3,5,4096,128]{3,2,1,0:T(8,128)(2,1)} %get-tuple-element.7.qk_ref.qkv_ref, f32[8,64,128]{2,1,0:T(8,128)} %get-tuple-element.8.ssq_ref, f32[2,5,128]{2,1,0:T(8,128)} %pad_maximum_fusion.gain_ref, f32[4096,128]{1,0:T(8,128)} %constant.9.clone.tab_ref), custom_call_target="tpu_custom_call" | custom-call | tf_op jit(solution)/shard_map/rotate_heads/pallas_call | solution.py:281
  225.5 201.3 %attend_scatter.1 = bf16[512,5120]{1,0:T(8,128)(2,1)} custom-call(bf16[5,8,512,128]{3,2,1,0:T(8,128)(2,1)} %bitcast.21, bf16[5,4096,128]{2,1,0:T(8,128)(2,1)} %get-tuple-element.10.k_ref, bf16[3,5,4096,128]{3,2,1,0:T(8,128)(2,1)} %get-tuple-element.7.qk_ref.qkv_ref, bf16[640,5120]{1,0:T(8,128)(2,1)} %wo_ref.1, bf16[512,5120]{1,0:T(8,128)(2,1)} %bitcast.16), custom_call_target="tpu_custom_call" | custom-call | tf_op jit(solution)/shard_map/attend_scatter/pallas_call | solution.py:508
  426.8 0.0 slice-start
  426.8 0.0 slice-start.1
  426.8 5.3 %slice_bitcast_fusion = bf16[1,4096,5,128]{3,1,2,0:T(8,128)(2,1)} fusion(bf16[3,5,4096,128]{3,2,1,0:T(8,128)(2,1)} %get-tuple-element.7.qk_ref.qkv_ref), kind=kLoop, calls=%fused_computation.5 | loop fusion | bytes 10485760 | tf_op jit(solution)/shard_map/broadcast_in_dim | solution.py:566
  432.2 0.0 slice-done
  432.2 0.0 slice-done.1
  432.2 2.4 copy.13
  (2 shorter events, 0.0 us)
Async XLA Ops:
  0.6 4.0 copy-start
  9.8 198.9 %copy-start.1 = (f32[640]{0:T(1024)S(1)}, f32[640]{0:T(1024)}, u32[]{:S(2)}) copy-start(f32[640]{0:T(1024)} %param.15) | copy-start | bytes 7684
  9.8 198.9 %copy-start.2 = (f32[640]{0:T(1024)S(1)}, f32[640]{0:T(1024)}, u32[]{:S(2)}) copy-start(f32[640]{0:T(1024)} %param.14) | copy-start | bytes 7684
  426.8 5.4 %slice-start = ((s8[5242880]{0:T(1024)(128)(4,1)}), s8[4194304]{0:T(1024)(128)(4,1)S(1)}, s32[]{:S(2)}) async-start(s8[5242880]{0:T(1024)(128)(4,1)} %bitcast.17), calls=%async_computation | async-start | bytes 8388608
  426.8 5.3 %slice-start.1 = ((s8[5242880]{0:T(1024)(128)(4,1)}), s8[1048576]{0:T(1024)(128)(4,1)S(1)}, s32[]{:S(2)}) async-start(s8[5242880]{0:T(1024)(128)(4,1)} %bitcast.17), calls=%async_computation.1 | async-start | bytes 2097152

commit v2 on v0

v2 whole, which is shorter than its diff:
```python
import functools

import jax
import jax.numpy as jnp
import numpy as np
from jax import lax
from jax.experimental import pallas as pl
from jax.experimental.pallas import tpu as pltpu
from jax.sharding import PartitionSpec as P

MESH = pl.DeviceIdType.MESH
HEAD_DIM = 128
HEADS = 5
COLS = HEADS * HEAD_DIM
WIDTH = 5120
BLOCK = 512
TP = 8
SEQ = TP * BLOCK
PIECES = 4
PIECE = BLOCK // PIECES
UNIT = 256
STEPS = 8
ROWS = BLOCK // STEPS
HALF = WIDTH // 2
TILE = 512
LAG = 4
WO_PARTS = 8
WO_ROWS = COLS // WO_PARTS
F32 = jnp.float32
BF16 = jnp.bfloat16
SIB, XN, YN, DG, SX, SY, SDG = range(7)


class Place:
    def __init__(self):
        me = lax.axis_index("tp")
        self.dp = lax.axis_index("dp")
        self.me = me
        self.core = me % 2
        self.x = (me // 2) % 2
        self.y = me // 4

    def at(self, fx, fy, fc):
        x = self.x + fx * (1 - 2 * self.x)
        y = self.y + fy * (1 - 2 * self.y)
        c = self.core + fc * (1 - 2 * self.core)
        return (y * 2 + x) * 2 + c

    def kind(self, k):
        fx, fy, fc = ((0, 0, 1), (1, 0, 0), (0, 1, 0), (1, 1, 0), (1, 0, 1), (0, 1, 1), (1, 1, 1))[k]
        return self.at(fx, fy, fc)

    def dev(self, index):
        return (self.dp, index)


def barrier_with(place, kinds):
    sem = pltpu.get_barrier_semaphore()
    for k in kinds:
        pl.semaphore_signal(sem, inc=1, device_id=place.dev(place.kind(k)), device_id_type=MESH)
    pl.semaphore_wait(sem, len(kinds))


def diagonal():
    r = lax.broadcasted_iota(jnp.int32, (128, 128), 0)
    c = lax.broadcasted_iota(jnp.int32, (128, 128), 1)
    return r == c


def block_kernel(h_ref, wq_ref, wk_ref, wv_ref, wo_ref, x_ref, gain_ref, tab_ref, out_ref, k_ref, v_ref, hbuf,
                 qkv, ssq_v, ssq_all, wr, o_in, recv0, r1,
                 w_sem, h_sem, send_sem, recv_sem, ss_send, ss_recv, ss_loc, kv_sem,
                 wo_send, wo_recv, wo_sem, tab_sem, o_send, o_recv, x_sem, out_sem, y_send, y_recv, s1_send, s1_recv):
    place = Place()
    scale = float(HEAD_DIM ** -0.5 * np.log2(np.e))
    eye = diagonal()
    weights = (wq_ref, wk_ref, wv_ref)

    def remote(src, dst, send, recv, kind):
        return pltpu.make_async_remote_copy(src_ref=src, dst_ref=dst, send_sem=send, recv_sem=recv,
                                            device_id=place.dev(place.kind(kind)), device_id_type=MESH)

    def copy(src_ref, block, p, send, kind, target):
        return remote(src_ref, hbuf.at[block, pl.ds(p * PIECE, PIECE)], send_sem.at[send, p], recv_sem.at[kind, p], target)

    def own(p, send, kind):
        return copy(h_ref.at[pl.ds(p * PIECE, PIECE)], place.me, p, send, kind, kind)

    def relay(owner, p, send, kind, target):
        block = place.kind(owner)
        return copy(hbuf.at[block, pl.ds(p * PIECE, PIECE)], block, p, send, kind, target)

    def arrived(kind, p):
        relay(kind, p, 0, kind, SIB).wait_recv()

    def forwards(p):
        out = [(XN, p, 3, SX, SIB), (YN, p, 4, SY, SIB)]
        out.append((XN, p, 5, DG, YN) if p % 2 == 0 else (YN, p, 5, DG, XN))
        return out

    def wo_part(c, half):
        rows = pl.ds(c * WO_ROWS, WO_ROWS)
        return remote(wo_ref.at[rows, pl.ds(half * HALF, HALF)], wr.at[half, rows],
                      wo_send.at[half, c], wo_recv.at[half, c], (XN, YN)[half])

    def share(k):
        return remote(ssq_v, ssq_all.at[place.me], ss_send.at[k], ss_recv.at[k], k)

    def shared(k):
        return remote(ssq_v, ssq_all.at[place.kind(k)], ss_send.at[k], ss_recv.at[k], k)

    def v_store():
        return pltpu.make_async_copy(qkv.at[2], v_ref, kv_sem.at[1])

    def k_store():
        return pltpu.make_async_copy(qkv.at[1], k_ref, kv_sem.at[0])

    def unit(u):
        a = u // 4
        v = u - 4
        w = v % 4
        z = u - 12
        near = a == 0
        far = a == 3
        fc = jnp.where(near, u // 2, jnp.where(far, z % 2, w // 2))
        half = jnp.where(near, u % 2, jnp.where(far, z // 2, v // 4))
        fy = jnp.where(near, 0, jnp.where(far, 1, w % 2))
        fx = jnp.where(near, 0, jnp.where(far, 1, 1 - w % 2))
        return place.at(fx, fy, fc), half

    def project_phase(w_v, h_v):
        for n, w in enumerate(weights):
            pltpu.make_async_copy(w, w_v.at[n], w_sem.at[n]).start()
        barrier_with(place, range(7))
        for p in range(PIECES):
            own(p, 0, XN).start()
            own(p, 1, YN).start()
            own(p, 2, SIB).start()

        def load(u, slot, own_rows):
            block, half = unit(u)
            rows = pl.ds(pl.multiple_of(half * UNIT, UNIT), UNIT)
            if own_rows:
                return pltpu.make_async_copy(h_ref.at[rows], h_v.at[slot], h_sem.at[slot])
            return pltpu.make_async_copy(hbuf.at[block, rows], h_v.at[slot], h_sem.at[slot])

        def start_load(u):
            @pl.when(u < 2)
            def _():
                load(u, u % 2, True).start()

            @pl.when(u >= 2)
            def _():
                load(u, u % 2, False).start()

        def step(u, carry):
            slot = u % 2
            for first, p0 in ((4, 0), (8, 2)):
                @pl.when(u == first)
                def _(p0=p0):
                    for p in (p0, p0 + 1):
                        arrived(XN, p)
                        arrived(YN, p)
                        for f in forwards(p):
                            relay(*f).start()
            for first, p0 in ((12, 0), (14, 2)):
                @pl.when(u == first)
                def _(p0=p0, first=first):
                    for p in (p0, p0 + 1):
                        arrived(DG, p)
                        relay(DG, p, 6, SDG, SIB).start()
                    if first == 14:
                        for half in range(2):
                            wo_part(0, half).start()

            @pl.when((u % 4 == 0) | (u == 14))
            def _():
                start_load(u)

            for nxt, kind, p0 in ((2, SIB, 0), (3, SIB, 2), (6, SX, 0), (7, SY, 0), (10, SX, 2), (11, SY, 2), (13, SDG, 0), (15, SDG, 2)):
                @pl.when(u + 1 == nxt)
                def _(kind=kind, p0=p0):
                    arrived(kind, p0)
                    arrived(kind, p0 + 1)

            @pl.when(((u + 1) % 4 != 0) & (u + 1 != 14))
            def _():
                start_load(u + 1)

            @pl.when(u == 0)
            def _():
                for n, w in enumerate(weights):
                    pltpu.make_async_copy(w, w_v.at[n], w_sem.at[n]).wait()

            load(u, slot, False).wait()
            block, half = unit(u)
            rows = pl.ds(pl.multiple_of(block * BLOCK + half * UNIT, UNIT), UNIT)

            def part(n, c):
                r = jnp.dot(h_v[slot], w_v[n], preferred_element_type=F32).astype(BF16)
                for h in range(HEADS):
                    qkv[n, h, rows, :] = r[:, h * HEAD_DIM:(h + 1) * HEAD_DIM]

                @pl.when(n < 2)
                def _():
                    rf = r.astype(F32)
                    col = jnp.sum(rf * rf, axis=1, keepdims=True)
                    for b in range(UNIT // 128):
                        row = jnp.sum(jnp.where(eye, col[b * 128:(b + 1) * 128], 0.0), axis=0, keepdims=True)
                        ssq_v[pl.ds(block * 8 + n * 4 + half * 2 + b, 1), :] = row
                return c

            lax.fori_loop(0, 3, part, 0)
            return carry

        lax.fori_loop(0, 16, step, 0)

    pl.run_scoped(project_phase, pltpu.VMEM((3, WIDTH, COLS), BF16), pltpu.VMEM((2, UNIT, WIDTH), BF16))

    for k in range(7):
        share(k).start()
    mine = pltpu.make_async_copy(ssq_v, ssq_all.at[place.me], ss_loc)
    mine.start()
    for c in range(1, WO_PARTS):
        for half in range(2):
            wo_part(c, half).start()
    v_store().start()

    def to_sib(ysend, s):
        return remote(ysend, recv0.at[s % 2], y_send, y_recv.at[s % 2], SIB)

    def hop(s1, s, half):
        b = s % 2
        return remote(s1.at[b, half], r1.at[b, half], s1_send.at[b, half], s1_recv.at[b, half], (YN, XN)[half])

    def o_part(o_v, s, half, n):
        chip = place.at(*((1, 0, 0), (0, 1, 0))[half]) // 2 if n == 0 else place.at(1, 1, 0) // 2
        rows = pl.ds(pl.multiple_of(chip * 2 * ROWS, 2 * ROWS), 2 * ROWS)
        return remote(o_v.at[s, rows], o_in.at[half, s, n], o_send.at[half, s, n], o_recv.at[half, s, n], (XN, YN)[half])

    def attend_phase(wo_v, o_v, tab_v, ysend, yown, s1, keep, x_v, ost):
        tab = pltpu.make_async_copy(tab_ref, tab_v, tab_sem)
        tab.start()

        def wo_load(half):
            return pltpu.make_async_copy(wo_ref.at[:, pl.ds(half * HALF, HALF)], wo_v.at[half], wo_sem.at[half])

        for half in range(2):
            wo_load(half).start()
        mine.wait()
        for k in range(7):
            shared(k).wait_recv()
        tab.wait()
        low = lax.broadcasted_iota(jnp.int32, (128, 128), 1) < 64

        def rotate(g, carry):
            rows = pl.ds(pl.multiple_of(g * 128, 128), 128)
            t = tab_v[rows, :]
            turned = pltpu.roll(t, 64, 1)
            cos = jnp.where(low, t, turned)
            sin = jnp.where(low, -turned, t)
            for n in range(2):
                at = g // 4 * 8 + n * 4 + g % 4
                total = jnp.sum(ssq_all[:, pl.ds(at, 1), :], axis=0)
                col = jnp.sum(jnp.where(eye, total, 0.0), axis=1, keepdims=True)
                inv = lax.rsqrt(col / WIDTH + 1e-5)
                for h in range(HEADS):
                    x = qkv[n, h, rows, :].astype(F32) * inv * gain_ref[n, h:h + 1, :]
                    qkv[n, h, rows, :] = (x * cos + pltpu.roll(x, 64, 1) * sin).astype(BF16)
            return carry

        lax.fori_loop(0, SEQ // 128, rotate, 0)
        k_store().start()

        def x_load(s):
            return pltpu.make_async_copy(x_ref.at[pl.ds(pl.multiple_of(s * ROWS, ROWS), ROWS)], x_v, x_sem)

        def out_store(s):
            return pltpu.make_async_copy(ost.at[s % 2], out_ref.at[pl.ds(pl.multiple_of(s * ROWS, ROWS), ROWS)], out_sem.at[s % 2])

        def tiles(body):
            def run(t, c):
                body(pl.ds(pl.multiple_of(t * TILE, TILE), TILE), t)
                return c
            lax.fori_loop(0, HALF // TILE, run, 0)

        def operand(s, half):
            rows = []
            for fc in (1, 0):
                for n, far in enumerate(((0, 0), ((0, 1), (1, 0))[half])):
                    d = place.at(far[0], far[1], fc)
                    mine_o = o_v[s, pl.ds(pl.multiple_of(d * ROWS, ROWS), ROWS), :]
                    theirs = o_in[half, s, n, pl.ds(pl.multiple_of(d % 2 * ROWS, ROWS), ROWS), :]
                    rows.append(jnp.concatenate([mine_o, theirs], axis=1))
            return jnp.concatenate(rows, axis=0)

        def stage_b(s):
            @pl.when(s == 0)
            def _():
                for half in range(2):
                    wo_load(half).wait()
                    for c in range(WO_PARTS):
                        wo_part(c, half).wait_recv()

            @pl.when(s >= 1)
            def _():
                to_sib(ysend, s - 1).wait_send()

            for half in range(2):
                for n in range(2):
                    o_part(o_v, s, half, n).wait_recv()
                rows = operand(s, half)

                def body(cols, t, half=half, rows=rows):
                    w = jnp.concatenate([wo_v[half, :, cols], wr[half, :, cols]], axis=0)
                    y = jnp.dot(rows, w, preferred_element_type=F32)
                    ysend[half, :, cols] = y[:2 * ROWS].astype(BF16)
                    yown[half, :, cols] = y[2 * ROWS:]
                tiles(body)
            to_sib(ysend, s).start()

        def stage_c(s):
            b = s % 2
            to_sib(ysend, s).wait_recv()

            @pl.when(s >= 2)
            def _():
                for half in range(2):
                    hop(s1, s - 2, half).wait_send()

            for half in range(2):
                def body(cols, t, half=half):
                    y = yown[half, :, cols] + recv0[b, half, :, cols].astype(F32)
                    keep[half, :, cols] = y[:ROWS]
                    s1[b, half, :, cols] = y[ROWS:].astype(BF16)
                tiles(body)
                hop(s1, s, half).start()

        def stage_d(s):
            b = s % 2
            x_load(s).wait()

            @pl.when(s >= 2)
            def _():
                out_store(s - 2).wait()

            for half in range(2):
                hop(s1, s, half).wait_recv()

                def body(cols, t, half=half):
                    y = (keep[half, :, cols] + r1[b, half, :, cols].astype(F32)).astype(BF16).astype(F32)
                    whole = pl.ds(pl.multiple_of(half * HALF + t * TILE, TILE), TILE)
                    ost[b, :, whole] = (x_v[:, whole].astype(F32) + y).astype(BF16)
                tiles(body)
            out_store(s).start()

        def attend(i, h):
            q = jnp.concatenate([qkv[0, h, pl.ds(pl.multiple_of(d * BLOCK + i * ROWS, ROWS), ROWS), :] for d in range(TP)], axis=0)
            dims = (((1,), (1,)), ((), ()))

            def scores(j):
                return lax.dot_general(q[j * ROWS:], qkv[1, h, j * BLOCK:(j + 1) * BLOCK, :], dims, preferred_element_type=F32)

            row = lax.broadcasted_iota(jnp.int32, (ROWS, BLOCK), 0) + i * ROWS
            keep_mask = lax.broadcasted_iota(jnp.int32, (ROWS, BLOCK), 1) <= row
            m = l = acc = None
            ahead = scores(0)
            for j in range(TP):
                s = ahead
                if j + 1 < TP:
                    ahead = scores(j + 1)
                top = jnp.where(keep_mask, s[:ROWS], -1e30)
                s = top if j == TP - 1 else jnp.concatenate([top, s[ROWS:]], axis=0)
                peak = jnp.max(s, axis=1, keepdims=True) * scale
                new_m = peak if j == 0 else jnp.maximum(m, peak)
                p = jnp.exp2(s * scale - new_m)
                part = p[:, 0:128]
                for c in range(1, BLOCK // 128):
                    part = part + p[:, c * 128:(c + 1) * 128]
                pv = jnp.dot(p.astype(BF16), qkv[2, h, j * BLOCK:(j + 1) * BLOCK, :], preferred_element_type=F32)
                if j == 0:
                    l, acc = part, pv
                else:
                    alpha = jnp.exp2(m - new_m)
                    l = l * alpha + part
                    acc = acc * alpha + pv
                total = jnp.sum(l[:ROWS], axis=1, keepdims=True)
                o_v[i, j * ROWS:(j + 1) * ROWS, pl.ds(pl.multiple_of(h * HEAD_DIM, HEAD_DIM), HEAD_DIM)] = (
                    acc[:ROWS] / total).astype(BF16)
                if j + 1 < TP:
                    m, l, acc = new_m[ROWS:], l[ROWS:], acc[ROWS:]

        def step(i, carry):
            d = i - LAG - 2
            c = i - LAG - 1

            @pl.when(d >= 0)
            def _():
                x_load(d).start()

            def head(h, z):
                @pl.when(h == 1)
                def _():
                    @pl.when(d >= 0)
                    def _():
                        stage_d(d)

                    @pl.when((c >= 0) & (c < STEPS))
                    def _():
                        stage_c(c)

                @pl.when(i < STEPS)
                def _():
                    attend(i, h)
                return z

            lax.fori_loop(0, HEADS, head, 0)

            @pl.when(i < STEPS)
            def _():
                for half in range(2):
                    for n in range(2):
                        o_part(o_v, i, half, n).start()

            @pl.when((i >= LAG) & (i < STEPS + LAG))
            def _():
                stage_b(i - LAG)
            return carry

        lax.fori_loop(0, STEPS + LAG + 2, step, 0)
        to_sib(ysend, STEPS - 1).wait_send()
        for s in (STEPS - 2, STEPS - 1):
            for half in range(2):
                hop(s1, s, half).wait_send()
            out_store(s).wait()
        for s in range(STEPS):
            for half in range(2):
                for n in range(2):
                    o_part(o_v, s, half, n).wait_send()

    pl.run_scoped(attend_phase,
                  pltpu.VMEM((2, COLS, HALF), BF16),
                  pltpu.VMEM((STEPS, BLOCK, COLS), BF16),
                  pltpu.VMEM((SEQ, 128), F32),
                  pltpu.VMEM((2, 2 * ROWS, HALF), BF16),
                  pltpu.VMEM((2, 2 * ROWS, HALF), F32),
                  pltpu.VMEM((2, 2, ROWS, HALF), BF16),
                  pltpu.VMEM((2, ROWS, HALF), F32),
                  pltpu.VMEM((ROWS, WIDTH), BF16),
                  pltpu.VMEM((2, ROWS, WIDTH), BF16))
    for p in range(PIECES):
        own(p, 0, XN).wait_send()
        own(p, 1, YN).wait_send()
        own(p, 2, SIB).wait_send()
        for f in forwards(p):
            relay(*f).wait_send()
        relay(DG, p, 6, SDG, SIB).wait_send()
    for k in range(7):
        share(k).wait_send()
    for half in range(2):
        for c in range(WO_PARTS):
            wo_part(c, half).wait_send()
    v_store().wait()
    k_store().wait()


def block_call(h, wq, wk, wv, wo, x, gains, table):
    any_spec = pl.BlockSpec(memory_space=pl.ANY)
    dma = pltpu.SemaphoreType.DMA
    return pl.pallas_call(
        block_kernel,
        out_shape=[jax.ShapeDtypeStruct((BLOCK, WIDTH), BF16),
                   jax.ShapeDtypeStruct((HEADS, SEQ, HEAD_DIM), BF16),
                   jax.ShapeDtypeStruct((HEADS, SEQ, HEAD_DIM), BF16),
                   jax.ShapeDtypeStruct((TP, BLOCK, WIDTH), BF16)],
        in_specs=[any_spec] * 6 + [pl.BlockSpec(memory_space=pltpu.VMEM), any_spec],
        out_specs=[any_spec] * 4,
        scratch_shapes=[
            pltpu.VMEM((3, HEADS, SEQ, HEAD_DIM), BF16),
            pltpu.VMEM((64, 128), F32),
            pltpu.VMEM((TP, 64, 128), F32),
            pltpu.VMEM((2, COLS, HALF), BF16),
            pltpu.VMEM((2, STEPS, 2, 2 * ROWS, COLS), BF16),
            pltpu.VMEM((2, 2, 2 * ROWS, HALF), BF16),
            pltpu.VMEM((2, 2, ROWS, HALF), BF16),
            dma((3,)), dma((2,)), dma((7, PIECES)), dma((7, PIECES)), dma((7,)), dma((7,)), dma(()), dma((2,)),
            dma((2, WO_PARTS)), dma((2, WO_PARTS)), dma((2,)), dma(()),
            dma((2, STEPS, 2)), dma((2, STEPS, 2)), dma(()), dma((2,)),
            dma(()), dma((2,)), dma((2, 2)), dma((2, 2)),
        ],
        compiler_params=pltpu.CompilerParams(collective_id=0, has_side_effects=True, vmem_limit_bytes=67043328),
        name="block",
    )(h, wq, wk, wv, wo, x, gains, table)


def rope_table():
    half = HEAD_DIM // 2
    freq = (10000.0 ** (-np.arange(half, dtype=np.float64) * (2.0 / HEAD_DIM))).astype(np.float32)
    angle = (np.arange(SEQ, dtype=np.float32)[:, None] * freq[None, :]).astype(np.float64)
    return np.concatenate([np.cos(angle), np.sin(angle)], axis=1).astype(np.float32)


def solution(mesh):
    table = rope_table()

    def local_block(x_local, attn_gain, wq, wk, wv, q_gain, k_gain, wo):
        x = x_local[0]
        xf = x.astype(F32)
        inv = lax.rsqrt(jnp.mean(xf * xf, axis=-1, keepdims=True) + 1e-5)
        h = (xf * inv * attn_gain).astype(BF16)
        gains = jnp.stack([q_gain, k_gain]).reshape(2, HEADS, HEAD_DIM)
        out, k, v, _ = block_call(h, wq, wk, wv, wo, x, gains, jnp.asarray(table))
        k_cache = jnp.transpose(k, (1, 0, 2))[None]
        v_cache = jnp.transpose(v, (1, 0, 2))[None]
        return out[None], k_cache, v_cache

    seq_spec = P("dp", "tp", None)
    head_spec = P("dp", None, "tp", None)
    col_spec = P(None, "tp")
    return jax.shard_map(local_block, mesh=mesh,
                         in_specs=(seq_spec, P(None), col_spec, col_spec, col_spec, P("tp"), P("tp"), P("tp", None)),
                         out_specs=(seq_spec, head_spec, head_spec), check_vma=False)
```

time: 1250 us -> 406 us (0.32)
  matrix products: 564 us -> 0 us
  Pallas kernels: 0 us -> 383 us
  waiting for transfers between devices: 376 us -> 0 us
  other arithmetic: 142 us -> 10.2 us
  local copies, waits for them, and re-layouts: 118 us -> 11.8 us
  blocking collectives: 22.6 us -> 0 us
  between operations: 15.5 us -> 0.67 us
    dot_general x67 -> x0, matrix products: 482 us -> none  [the longest x32 197 us: causal_attention(): jnp.einsum('bhqk,bkhd->bqhd', prob_bf, v_heads[:, :q_stop], preferred_ele...]
    pallas_call x0 -> x1, Pallas kernels: none -> 383 us  [block_call(): pl.pallas_call(block_kernel, out_shape=[jax.ShapeDtypeStruct((BLOCK, WIDT...]
    unnamed x3 -> x0, waiting for transfers between devices: 220 us -> none
    all_gather x1 -> x0, waiting for transfers between devices: 155 us -> none  [local_block(): h_full = lax.all_gather(normed, 'tp', axis=1, tiled=True)]
    unnamed x262 -> x11, local copies, waits for them, and re-layouts: 109 us -> 11.8 us
    sub x18 -> x0, matrix products: 82 us -> none  [causal_attention(): prob_bf = jax.nn.softmax(scores, axis=-1).astype(jnp.bfloat16)]
    sub x14 -> x0, other arithmetic: 31.6 us -> none  [causal_attention(): prob_bf = jax.nn.softmax(scores, axis=-1).astype(jnp.bfloat16)]
    ge x32 -> x0, other arithmetic: 29.4 us -> none  [causal_attention(): scores = jnp.where(q_pos[:, None] >= k_pos[None, :], scores, -1e+30)]
  transfers between devices with their start and end apart: 2 -> 0, of which waited for: 2 -> 0; matrix products, arithmetic and copies ran while one was open for 5% -> 0% of each run, Pallas kernels for 0% -> 0%
where the time goes in v2:
time: 406 us
  Pallas kernels  383 us (94%)
  local copies, waits for them, and re-layouts  11.8 us (3%)
  other arithmetic  10.2 us (3%)
    pallas_call x1, Pallas kernels, block_call(): pl.pallas_call(block_kernel, out_shape=[jax.ShapeDtypeStruct((BLOCK, WIDT...  383 us
    unnamed x11, local copies, waits for them, and re-layouts  11.8 us

profile of v2, /device:TPU:0, one launch (start us, length us, event | category | flops | bytes accessed | tf_op | source)
XLA Modules:
  0.0 405.9 jit_solution(13708126634197479522)
XLA Ops:
  0.6 0.0 copy-start
  0.6 3.7 fusion
  4.4 1.3 pad_maximum_fusion.gain_ref
  5.7 0.0 copy-done
  5.7 5.1 %fusion.2.h_ref = bf16[512,5120]{1,0:T(8,128)(2,1)} fusion(f32[5120]{0:T(1024)} %param.10, f32[512]{0:T(512)S(1)} %add_rsqrt_fusion, bf16[1,512,5120]{2,1,0:T(8,128)(2,1)S(1)} %copy-done), kind=kLoop, calls=%fused_computation.4 | loop fusion | flops 10485760 | bytes 10508288 | tf_op jit(solution)/shard_map/convert_element_type | solution.py:510
  10.8 383.2 %block.1 = (bf16[512,5120]{1,0:T(8,128)(2,1)}, bf16[5,4096,128]{2,1,0:T(8,128)(2,1)}, bf16[5,4096,128]{2,1,0:T(8,128)(2,1)}, bf16[8,512,5120]{2,1,0:T(8,128)(2,1)}) custom-call(bf16[512,5120]{1,0:T(8,128)(2,1)} %fusion.2.h_ref, bf16[5120,640]{1,0:T(8,128)(2,1)} %wq_ref.1, bf16[5120,640]{1,0:T(8,128)(2,1)} %wk_ref.1, bf16[5120,640]{1,0:T(8,128)(2,1)} %wv_ref.1, ...), custom_call_target="tpu_custom_call" | custom-call | tf_op jit(solution)/shard_map/block/pallas_call | solution.py:470
  394.1 0.0 copy-start.1
  394.1 0.0 slice-start
  394.1 5.7 %copy.15 = bf16[1,512,5120]{2,1,0:T(8,128)(2,1)} copy(bf16[1,512,5120]{2,1,0:T(8,128)(2,1)} %bitcast.17) | data formatting | bytes 10485760
  399.7 0.0 copy-done.1
  399.7 0.0 slice-start.1
  399.7 2.7 copy.16
  402.4 0.1 slice-done
  402.5 1.0 slice-done.1
  403.5 2.4 copy.17
  (2 shorter events, 0.0 us)
Async XLA Ops:
  0.6 5.1 %copy-start = (bf16[1,512,5120]{2,1,0:T(8,128)(2,1)S(1)}, bf16[1,512,5120]{2,1,0:T(8,128)(2,1)}, u32[]{:S(2)}) copy-start(bf16[1,512,5120]{2,1,0:T(8,128)(2,1)} %param.9) | copy-start | bytes 15728644
  394.1 5.7 %copy-start.1 = (bf16[5,4096,128]{2,1,0:T(8,128)(2,1)S(1)}, bf16[5,4096,128]{2,1,0:T(8,128)(2,1)}, u32[]{:S(2)}) copy-start(bf16[5,4096,128]{2,1,0:T(8,128)(2,1)} %get-tuple-element.7) | copy-start | bytes 15728644
  394.1 8.4 %slice-start = ((s8[5242880]{0:T(1024)(128)(4,1)}), s8[4194304]{0:T(1024)(128)(4,1)S(1)}, s32[]{:S(2)}) async-start(s8[5242880]{0:T(1024)(128)(4,1)} %bitcast.13), calls=%async_computation | async-start | bytes 8388608
  399.7 3.8 slice-start.1

commit v3 on v2

--- a/solution.py
+++ b/solution.py
@@ -16,15 +16,16 @@
 BLOCK = 512
 TP = 8
 SEQ = TP * BLOCK
-PIECES = 4
+PIECES = 8
 PIECE = BLOCK // PIECES
-UNIT = 256
+UNIT = 128
 STEPS = 8
 ROWS = BLOCK // STEPS
 HALF = WIDTH // 2
 TILE = 512
 LAG = 4
-WO_PARTS = 8
+EARLY = 2
+WO_PARTS = 10
 WO_ROWS = COLS // WO_PARTS
 F32 = jnp.float32
 BF16 = jnp.bfloat16
@@ -54,11 +55,13 @@
         return (self.dp, index)
 
 
-def barrier_with(place, kinds):
-    sem = pltpu.get_barrier_semaphore()
+def barrier_signal(place, kinds):
     for k in kinds:
-        pl.semaphore_signal(sem, inc=1, device_id=place.dev(place.kind(k)), device_id_type=MESH)
-    pl.semaphore_wait(sem, len(kinds))
+        pl.semaphore_signal(pltpu.get_barrier_semaphore(), inc=1, device_id=place.dev(place.kind(k)), device_id_type=MESH)
+
+
+def barrier_wait(count):
+    pl.semaphore_wait(pltpu.get_barrier_semaphore(), count)
 
 
 def diagonal():
@@ -67,9 +70,9 @@
     return r == c
 
 
-def block_kernel(h_ref, wq_ref, wk_ref, wv_ref, wo_ref, x_ref, gain_ref, tab_ref, out_ref, k_ref, v_ref, hbuf,
+def block_kernel(x_ref, an_ref, wq_ref, wk_ref, wv_ref, qg_ref, kg_ref, wo_ref, tab_ref, out_ref, k_ref, v_ref, hbuf,
                  qkv, ssq_v, ssq_all, wr, o_in, recv0, r1,
-                 w_sem, h_sem, send_sem, recv_sem, ss_send, ss_recv, ss_loc, kv_sem,
+                 w_sem, h_sem, n_sem, send_sem, recv_sem, ss_send, ss_recv, ss_loc, kv_sem,
                  wo_send, wo_recv, wo_sem, tab_sem, o_send, o_recv, x_sem, out_sem, y_send, y_recv, s1_send, s1_recv):
     place = Place()
     scale = float(HEAD_DIM ** -0.5 * np.log2(np.e))
@@ -84,7 +87,7 @@
         return remote(src_ref, hbuf.at[block, pl.ds(p * PIECE, PIECE)], send_sem.at[send, p], recv_sem.at[kind, p], target)
 
     def own(p, send, kind):
-        return copy(h_ref.at[pl.ds(p * PIECE, PIECE)], place.me, p, send, kind, kind)
+        return copy(hbuf.at[place.me, pl.ds(p * PIECE, PIECE)], place.me, p, send, kind, kind)
 
     def relay(owner, p, send, kind, target):
         block = place.kind(owner)
@@ -116,74 +119,94 @@
         return pltpu.make_async_copy(qkv.at[1], k_ref, kv_sem.at[0])
 
     def unit(u):
-        a = u // 4
-        v = u - 4
+        v = u - 8
         w = v % 4
-        z = u - 12
-        near = a == 0
-        far = a == 3
-        fc = jnp.where(near, u // 2, jnp.where(far, z % 2, w // 2))
-        half = jnp.where(near, u % 2, jnp.where(far, z // 2, v // 4))
+        z = u - 24
+        near = u < 8
+        far = u >= 24
+        fc = jnp.where(near, u // 4, jnp.where(far, z % 2, w // 2))
+        part = jnp.where(near, u % 4, jnp.where(far, z // 2, v // 4))
         fy = jnp.where(near, 0, jnp.where(far, 1, w % 2))
         fx = jnp.where(near, 0, jnp.where(far, 1, 1 - w % 2))
-        return place.at(fx, fy, fc), half
+        return place.at(fx, fy, fc), part
 
     def project_phase(w_v, h_v):
+        def x_piece(p):
+            return pltpu.make_async_copy(x_ref.at[pl.ds(p * PIECE, PIECE)], h_v.at[1, pl.ds(p % 2 * PIECE, PIECE)], n_sem.at[0, p % 2])
+
+        def h_piece(p):
+            return pltpu.make_async_copy(h_v.at[0, pl.ds(p % 2 * PIECE, PIECE)], hbuf.at[place.me, pl.ds(p * PIECE, PIECE)], n_sem.at[1, p % 2])
+
+        x_piece(0).start()
+        x_piece(1).start()
         for n, w in enumerate(weights):
             pltpu.make_async_copy(w, w_v.at[n], w_sem.at[n]).start()
-        barrier_with(place, range(7))
+        barrier_signal(place, range(7))
         for p in range(PIECES):
+            x_piece(p).wait()
+
+            def normalize(r, c, p=p):
+                rows = pl.ds(pl.multiple_of(p % 2 * PIECE + r * 16, 16), 16)
+                xf = h_v[1, rows, :].astype(F32)
+                inv = lax.rsqrt(jnp.mean(xf * xf, axis=-1, keepdims=True) + 1e-5)
+                h_v[0, rows, :] = (xf * inv * an_ref[...]).astype(BF16)
+                return c
+
+            lax.fori_loop(0, PIECE // 16, normalize, 0)
+            h_piece(p).start()
+            if p + 2 < PIECES:
+                x_piece(p + 2).start()
+            h_piece(p).wait()
+            if p == 0:
+                barrier_wait(7)
             own(p, 0, XN).start()
             own(p, 1, YN).start()
             own(p, 2, SIB).start()
 
-        def load(u, slot, own_rows):
+        def load(u, slot):
             block, half = unit(u)
             rows = pl.ds(pl.multiple_of(half * UNIT, UNIT), UNIT)
-            if own_rows:
-                return pltpu.make_async_copy(h_ref.at[rows], h_v.at[slot], h_sem.at[slot])
             return pltpu.make_async_copy(hbuf.at[block, rows], h_v.at[slot], h_sem.at[slot])
 
         def start_load(u):
-            @pl.when(u < 2)
-            def _():
-                load(u, u % 2, True).start()
-
-            @pl.when(u >= 2)
-            def _():
-                load(u, u % 2, False).start()
+            load(u, u % 2).start()
 
         def step(u, carry):
             slot = u % 2
-            for first, p0 in ((4, 0), (8, 2)):
-                @pl.when(u == first)
-                def _(p0=p0):
-                    for p in (p0, p0 + 1):
+            for g in range(4):
+                @pl.when(u == 8 + 4 * g)
+                def _(g=g):
+                    for p in (2 * g, 2 * g + 1):
                         arrived(XN, p)
                         arrived(YN, p)
                         for f in forwards(p):
                             relay(*f).start()
-            for first, p0 in ((12, 0), (14, 2)):
-                @pl.when(u == first)
-                def _(p0=p0, first=first):
-                    for p in (p0, p0 + 1):
+
+                @pl.when(u == 24 + 2 * g)
+                def _(g=g):
+                    for p in (2 * g, 2 * g + 1):
                         arrived(DG, p)
                         relay(DG, p, 6, SDG, SIB).start()
-                    if first == 14:
-                        for half in range(2):
-                            wo_part(0, half).start()
-
-            @pl.when((u % 4 == 0) | (u == 14))
+                    if g == 2:
+                        for c in range(EARLY):
+                            for half in range(2):
+                                wo_part(c, half).start()
+
+            def opens(t):
+                return (t == 0) | ((t >= 8) & (t < 24) & (t % 4 == 0)) | ((t >= 24) & (t % 2 == 0))
+
+            @pl.when(opens(u))
             def _():
                 start_load(u)
 
-            for nxt, kind, p0 in ((2, SIB, 0), (3, SIB, 2), (6, SX, 0), (7, SY, 0), (10, SX, 2), (11, SY, 2), (13, SDG, 0), (15, SDG, 2)):
-                @pl.when(u + 1 == nxt)
-                def _(kind=kind, p0=p0):
-                    arrived(kind, p0)
-                    arrived(kind, p0 + 1)
-
-            @pl.when(((u + 1) % 4 != 0) & (u + 1 != 14))
+            for g in range(4):
+                for nxt, kind in ((4 + g, SIB), (10 + 4 * g, SX), (11 + 4 * g, SY), (25 + 2 * g, SDG)):
+                    @pl.when(u + 1 == nxt)
+                    def _(kind=kind, g=g):
+                        arrived(kind, 2 * g)
+                        arrived(kind, 2 * g + 1)
+
+            @pl.when((u + 1 < 32) & jnp.logical_not(opens(u + 1)))
             def _():
                 start_load(u + 1)
 
@@ -192,7 +215,7 @@
                 for n, w in enumerate(weights):
                     pltpu.make_async_copy(w, w_v.at[n], w_sem.at[n]).wait()
 
-            load(u, slot, False).wait()
+            load(u, slot).wait()
             block, half = unit(u)
             rows = pl.ds(pl.multiple_of(block * BLOCK + half * UNIT, UNIT), UNIT)
 
@@ -207,13 +230,13 @@
                     col = jnp.sum(rf * rf, axis=1, keepdims=True)
                     for b in range(UNIT // 128):
                         row = jnp.sum(jnp.where(eye, col[b * 128:(b + 1) * 128], 0.0), axis=0, keepdims=True)
-                        ssq_v[pl.ds(block * 8 + n * 4 + half * 2 + b, 1), :] = row
+                        ssq_v[pl.ds(block * 8 + n * 4 + half, 1), :] = row
                 return c
 
             lax.fori_loop(0, 3, part, 0)
             return carry
 
-        lax.fori_loop(0, 16, step, 0)
+        lax.fori_loop(0, 32, step, 0)
 
     pl.run_scoped(project_phase, pltpu.VMEM((3, WIDTH, COLS), BF16), pltpu.VMEM((2, UNIT, WIDTH), BF16))
 
@@ -221,7 +244,7 @@
         share(k).start()
     mine = pltpu.make_async_copy(ssq_v, ssq_all.at[place.me], ss_loc)
     mine.start()
-    for c in range(1, WO_PARTS):
+    for c in range(EARLY, WO_PARTS):
         for half in range(2):
             wo_part(c, half).start()
     v_store().start()
@@ -231,7 +254,7 @@
 
     def hop(s1, s, half):
         b = s % 2
-        return remote(s1.at[b, half], r1.at[b, half], s1_send.at[b, half], s1_recv.at[b, half], (YN, XN)[half])
+        return remote(s1.at[b, half], r1.at[s % 4, half], s1_send.at[b, half], s1_recv.at[s % 4, half], (YN, XN)[half])
 
     def o_part(o_v, s, half, n):
         chip = place.at(*((1, 0, 0), (0, 1, 0))[half]) // 2 if n == 0 else place.at(1, 1, 0) // 2
@@ -252,6 +275,7 @@
             shared(k).wait_recv()
         tab.wait()
         low = lax.broadcasted_iota(jnp.int32, (128, 128), 1) < 64
+        gains = [[g[h * HEAD_DIM:(h + 1) * HEAD_DIM][None] for h in range(HEADS)] for g in (qg_ref, kg_ref)]
 
         def rotate(g, carry):
             rows = pl.ds(pl.multiple_of(g * 128, 128), 128)
@@ -265,11 +289,11 @@
                 col = jnp.sum(jnp.where(eye, total, 0.0), axis=1, keepdims=True)
                 inv = lax.rsqrt(col / WIDTH + 1e-5)
                 for h in range(HEADS):
-                    x = qkv[n, h, rows, :].astype(F32) * inv * gain_ref[n, h:h + 1, :]
+                    x = qkv[n, h, rows, :].astype(F32) * inv * gains[n][h]
                     qkv[n, h, rows, :] = (x * cos + pltpu.roll(x, 64, 1) * sin).astype(BF16)
             return carry
 
-        lax.fori_loop(0, SEQ // 128, rotate, 0)
+        lax.fori_loop(0, SEQ // 128, rotate, 0, unroll=2)
         k_store().start()
 
         def x_load(s):
@@ -331,7 +355,7 @@
             for half in range(2):
                 def body(cols, t, half=half):
                     y = yown[half, :, cols] + recv0[b, half, :, cols].astype(F32)
-                    keep[half, :, cols] = y[:ROWS]
+                    keep[b, half, :, cols] = y[:ROWS]
                     s1[b, half, :, cols] = y[ROWS:].astype(BF16)
                 tiles(body)
                 hop(s1, s, half).start()
@@ -348,7 +372,7 @@
                 hop(s1, s, half).wait_recv()
 
                 def body(cols, t, half=half):
-                    y = (keep[half, :, cols] + r1[b, half, :, cols].astype(F32)).astype(BF16).astype(F32)
+                    y = (keep[b, half, :, cols] + r1[s % 4, half, :, cols].astype(F32)).astype(BF16).astype(F32)
                     whole = pl.ds(pl.multiple_of(half * HALF + t * TILE, TILE), TILE)
                     ost[b, :, whole] = (x_v[:, whole].astype(F32) + y).astype(BF16)
                 tiles(body)
@@ -390,44 +414,44 @@
                 if j + 1 < TP:
                     m, l, acc = new_m[ROWS:], l[ROWS:], acc[ROWS:]
 
+        def substep(s):
+            @pl.when((s >= 3) & (s < STEPS + 3))
+            def _():
+                stage_d(s - 3)
+
+            @pl.when((s >= 2) & (s < STEPS + 2))
+            def _():
+                x_load(s - 2).start()
+
+            @pl.when((s >= 1) & (s <= STEPS))
+            def _():
+                stage_c(s - 1)
+
+            @pl.when((s >= 0) & (s < STEPS))
+            def _():
+                stage_b(s)
+
         def step(i, carry):
-            d = i - LAG - 2
-            c = i - LAG - 1
-
-            @pl.when(d >= 0)
-            def _():
-                x_load(d).start()
-
             def head(h, z):
-                @pl.when(h == 1)
-                def _():
-                    @pl.when(d >= 0)
-                    def _():
-                        stage_d(d)
-
-                    @pl.when((c >= 0) & (c < STEPS))
-                    def _():
-                        stage_c(c)
-
                 @pl.when(i < STEPS)
                 def _():
                     attend(i, h)
+
+                    @pl.when(h == HEADS - 1)
+                    def _():
+                        for half in range(2):
+                            for n in range(2):
+                                o_part(o_v, i, half, n).start()
+
+                @pl.when((i >= LAG) & ((h == 1) | (h == HEADS - 1)))
+                def _():
+                    substep(2 * (i - LAG) + h // (HEADS - 1) - 1)
                 return z
 
             lax.fori_loop(0, HEADS, head, 0)
-
-            @pl.when(i < STEPS)
-            def _():
-                for half in range(2):
-                    for n in range(2):
-                        o_part(o_v, i, half, n).start()
-
-            @pl.when((i >= LAG) & (i < STEPS + LAG))
-            def _():
-                stage_b(i - LAG)
             return carry
 
-        lax.fori_loop(0, STEPS + LAG + 2, step, 0)
+        lax.fori_loop(0, LAG + STEPS // 2 + 2, step, 0)
         to_sib(ysend, STEPS - 1).wait_send()
         for s in (STEPS - 2, STEPS - 1):
             for half in range(2):
@@ -445,7 +469,7 @@
                   pltpu.VMEM((2, 2 * ROWS, HALF), BF16),
                   pltpu.VMEM((2, 2 * ROWS, HALF), F32),
                   pltpu.VMEM((2, 2, ROWS, HALF), BF16),
-                  pltpu.VMEM((2, ROWS, HALF), F32),
+                  pltpu.VMEM((2, 2, ROWS, HALF), F32),
                   pltpu.VMEM((ROWS, WIDTH), BF16),
                   pltpu.VMEM((2, ROWS, WIDTH), BF16))
     for p in range(PIECES):
@@ -464,8 +488,9 @@
     k_store().wait()
 
 
-def block_call(h, wq, wk, wv, wo, x, gains, table):
+def block_call(x, an, wq, wk, wv, qg, kg, wo, table):
     any_spec = pl.BlockSpec(memory_space=pl.ANY)
+    vmem_spec = pl.BlockSpec(memory_space=pltpu.VMEM)
     dma = pltpu.SemaphoreType.DMA
     return pl.pallas_call(
         block_kernel,
@@ -473,7 +498,7 @@
                    jax.ShapeDtypeStruct((HEADS, SEQ, HEAD_DIM), BF16),
                    jax.ShapeDtypeStruct((HEADS, SEQ, HEAD_DIM), BF16),
                    jax.ShapeDtypeStruct((TP, BLOCK, WIDTH), BF16)],
-        in_specs=[any_spec] * 6 + [pl.BlockSpec(memory_space=pltpu.VMEM), any_spec],
+        in_specs=[any_spec, vmem_spec, any_spec, any_spec, any_spec, vmem_spec, vmem_spec, any_spec, any_spec],
         out_specs=[any_spec] * 4,
         scratch_shapes=[
             pltpu.VMEM((3, HEADS, SEQ, HEAD_DIM), BF16),
@@ -482,15 +507,15 @@
             pltpu.VMEM((2, COLS, HALF), BF16),
             pltpu.VMEM((2, STEPS, 2, 2 * ROWS, COLS), BF16),
             pltpu.VMEM((2, 2, 2 * ROWS, HALF), BF16),
-            pltpu.VMEM((2, 2, ROWS, HALF), BF16),
-            dma((3,)), dma((2,)), dma((7, PIECES)), dma((7, PIECES)), dma((7,)), dma((7,)), dma(()), dma((2,)),
+            pltpu.VMEM((4, 2, ROWS, HALF), BF16),
+            dma((3,)), dma((2,)), dma((2, 2)), dma((7, PIECES)), dma((7, PIECES)), dma((7,)), dma((7,)), dma(()), dma((2,)),
             dma((2, WO_PARTS)), dma((2, WO_PARTS)), dma((2,)), dma(()),
             dma((2, STEPS, 2)), dma((2, STEPS, 2)), dma(()), dma((2,)),
-            dma(()), dma((2,)), dma((2, 2)), dma((2, 2)),
+            dma(()), dma((2,)), dma((2, 2)), dma((4, 2)),
         ],
         compiler_params=pltpu.CompilerParams(collective_id=0, has_side_effects=True, vmem_limit_bytes=67043328),
         name="block",
-    )(h, wq, wk, wv, wo, x, gains, table)
+    )(x, an, wq, wk, wv, qg, kg, wo, table)
 
 
 def rope_table():
@@ -504,12 +529,7 @@
     table = rope_table()
 
     def local_block(x_local, attn_gain, wq, wk, wv, q_gain, k_gain, wo):
-        x = x_local[0]
-        xf = x.astype(F32)
-        inv = lax.rsqrt(jnp.mean(xf * xf, axis=-1, keepdims=True) + 1e-5)
-        h = (xf * inv * attn_gain).astype(BF16)
-        gains = jnp.stack([q_gain, k_gain]).reshape(2, HEADS, HEAD_DIM)
-        out, k, v, _ = block_call(h, wq, wk, wv, wo, x, gains, jnp.asarray(table))
+        out, k, v, _ = block_call(x_local[0], attn_gain[None], wq, wk, wv, q_gain, k_gain, wo, jnp.asarray(table))
         k_cache = jnp.transpose(k, (1, 0, 2))[None]
         v_cache = jnp.transpose(v, (1, 0, 2))[None]
         return out[None], k_cache, v_cache

time: 406 us -> 378 us (0.931)
  Pallas kernels: 383 us -> 365 us
  other arithmetic: 10.2 us -> 0.01 us
    pallas_call x1, Pallas kernels: 383 us -> 365 us  [block_call(): pl.pallas_call(block_kernel, out_shape=[jax.ShapeDtypeStruct((BLOCK, WIDT...]
    convert_element_type x1 -> x0, other arithmetic: 5.11 us -> none  [local_block(): h = (xf * inv * attn_gain).astype(BF16)]
    unnamed x11 -> x9, local copies, waits for them, and re-layouts: 11.8 us -> 11.8 us
where the time goes in v3:
time: 378 us; the launch traced here: 377 us
  Pallas kernels  365 us (97%)
  local copies, waits for them, and re-layouts  11.8 us (3%)
    pallas_call x1, Pallas kernels, block_call(): pl.pallas_call(block_kernel, out_shape=[jax.ShapeDtypeStruct((BLOCK, WIDT...  365 us
    unnamed x9, local copies, waits for them, and re-layouts  11.8 us

profile of v3, /device:TPU:0, one launch (start us, length us, event | category | flops | bytes accessed | tf_op | source)
XLA Modules:
  0.0 377.5 jit_solution(271307413162295317)
XLA Ops:
  0.6 365.0 %block.1 = (bf16[512,5120]{1,0:T(8,128)(2,1)}, bf16[5,4096,128]{2,1,0:T(8,128)(2,1)}, bf16[5,4096,128]{2,1,0:T(8,128)(2,1)}, bf16[8,512,5120]{2,1,0:T(8,128)(2,1)}) custom-call(bf16[512,5120]{1,0:T(8,128)(2,1)} %bitcast.9, f32[1,5120]{1,0:T(1,128)} %bitcast.15, bf16[5120,640]{1,0:T(8,128)(2,1)} %wq_ref.1, bf16[5120,640]{1,0:T(8,128)(2,1)} %wk_ref.1, ...), custom_call_target="tpu_custom_call" | custom-call | tf_op jit(solution)/shard_map/block/pallas_call | solution.py:495
  365.7 0.0 copy-start
  365.7 0.0 slice-start
  365.7 5.7 %copy.15 = bf16[1,512,5120]{2,1,0:T(8,128)(2,1)} copy(bf16[1,512,5120]{2,1,0:T(8,128)(2,1)} %bitcast.14) | data formatting | bytes 10485760
  371.4 0.0 copy-done
  371.4 0.0 slice-start.1
  371.4 2.7 copy.16
  374.0 0.1 slice-done
  374.1 1.0 slice-done.1
  375.1 2.4 copy.17
  (1 shorter events, 0.0 us)
Async XLA Ops:
  365.7 5.7 %copy-start = (bf16[5,4096,128]{2,1,0:T(8,128)(2,1)S(1)}, bf16[5,4096,128]{2,1,0:T(8,128)(2,1)}, u32[]{:S(2)}) copy-start(bf16[5,4096,128]{2,1,0:T(8,128)(2,1)} %get-tuple-element.7) | copy-start | bytes 15728644
  365.7 8.4 %slice-start = ((s8[5242880]{0:T(1024)(128)(4,1)}), s8[4194304]{0:T(1024)(128)(4,1)S(1)}, s32[]{:S(2)}) async-start(s8[5242880]{0:T(1024)(128)(4,1)} %bitcast.10), calls=%async_computation | async-start | bytes 8388608
  371.4 3.8 slice-start.1

commit v4 on v3

--- a/solution.py
+++ b/solution.py
@@ -71,9 +71,9 @@
 
 
 def block_kernel(x_ref, an_ref, wq_ref, wk_ref, wv_ref, qg_ref, kg_ref, wo_ref, tab_ref, out_ref, k_ref, v_ref, hbuf,
-                 qkv, ssq_v, ssq_all, wr, o_in, recv0, r1,
-                 w_sem, h_sem, n_sem, send_sem, recv_sem, ss_send, ss_recv, ss_loc, kv_sem,
-                 wo_send, wo_recv, wo_sem, tab_sem, o_send, o_recv, x_sem, out_sem, y_send, y_recv, s1_send, s1_recv):
+                 q_ref, ssq_v, ssq_all, wr, o_in, recv0, r1,
+                 w_sem, h_sem, n_sem, send_sem, recv_sem, ss_send, ss_recv, ss_loc,
+                 wo_send, wo_recv, wo_sem, tab_sem, o_send, o_recv, x_sem, y_send, y_recv, s1_send, s1_recv):
     place = Place()
     scale = float(HEAD_DIM ** -0.5 * np.log2(np.e))
     eye = diagonal()
@@ -112,11 +112,7 @@
     def shared(k):
         return remote(ssq_v, ssq_all.at[place.kind(k)], ss_send.at[k], ss_recv.at[k], k)
 
-    def v_store():
-        return pltpu.make_async_copy(qkv.at[2], v_ref, kv_sem.at[1])
-
-    def k_store():
-        return pltpu.make_async_copy(qkv.at[1], k_ref, kv_sem.at[0])
+    qkv = (q_ref, k_ref, v_ref)
 
     def unit(u):
         v = u - 8
@@ -221,8 +217,11 @@
 
             def part(n, c):
                 r = jnp.dot(h_v[slot], w_v[n], preferred_element_type=F32).astype(BF16)
-                for h in range(HEADS):
-                    qkv[n, h, rows, :] = r[:, h * HEAD_DIM:(h + 1) * HEAD_DIM]
+                for m in range(3):
+                    @pl.when(n == m)
+                    def _(m=m):
+                        for h in range(HEADS):
+                            qkv[m][h, rows, :] = r[:, h * HEAD_DIM:(h + 1) * HEAD_DIM]
 
                 @pl.when(n < 2)
                 def _():
@@ -247,7 +246,6 @@
     for c in range(EARLY, WO_PARTS):
         for half in range(2):
             wo_part(c, half).start()
-    v_store().start()
 
     def to_sib(ysend, s):
         return remote(ysend, recv0.at[s % 2], y_send, y_recv.at[s % 2], SIB)
@@ -261,7 +259,7 @@
         rows = pl.ds(pl.multiple_of(chip * 2 * ROWS, 2 * ROWS), 2 * ROWS)
         return remote(o_v.at[s, rows], o_in.at[half, s, n], o_send.at[half, s, n], o_recv.at[half, s, n], (XN, YN)[half])
 
-    def attend_phase(wo_v, o_v, tab_v, ysend, yown, s1, keep, x_v, ost):
+    def attend_phase(wo_v, o_v, tab_v, ysend, yown, s1, keep, x_v):
         tab = pltpu.make_async_copy(tab_ref, tab_v, tab_sem)
         tab.start()
 
@@ -289,18 +287,14 @@
                 col = jnp.sum(jnp.where(eye, total, 0.0), axis=1, keepdims=True)
                 inv = lax.rsqrt(col / WIDTH + 1e-5)
                 for h in range(HEADS):
-                    x = qkv[n, h, rows, :].astype(F32) * inv * gains[n][h]
-                    qkv[n, h, rows, :] = (x * cos + pltpu.roll(x, 64, 1) * sin).astype(BF16)
+                    x = qkv[n][h, rows, :].astype(F32) * inv * gains[n][h]
+                    qkv[n][h, rows, :] = (x * cos + pltpu.roll(x, 64, 1) * sin).astype(BF16)
             return carry
 
         lax.fori_loop(0, SEQ // 128, rotate, 0, unroll=2)
-        k_store().start()
 
         def x_load(s):
             return pltpu.make_async_copy(x_ref.at[pl.ds(pl.multiple_of(s * ROWS, ROWS), ROWS)], x_v, x_sem)
-
-        def out_store(s):
-            return pltpu.make_async_copy(ost.at[s % 2], out_ref.at[pl.ds(pl.multiple_of(s * ROWS, ROWS), ROWS)], out_sem.at[s % 2])
 
         def tiles(body):
             def run(t, c):
@@ -364,26 +358,21 @@
             b = s % 2
             x_load(s).wait()
 
-            @pl.when(s >= 2)
-            def _():
-                out_store(s - 2).wait()
-
             for half in range(2):
                 hop(s1, s, half).wait_recv()
 
                 def body(cols, t, half=half):
                     y = (keep[b, half, :, cols] + r1[s % 4, half, :, cols].astype(F32)).astype(BF16).astype(F32)
                     whole = pl.ds(pl.multiple_of(half * HALF + t * TILE, TILE), TILE)
-                    ost[b, :, whole] = (x_v[:, whole].astype(F32) + y).astype(BF16)
+                    out_ref[pl.ds(pl.multiple_of(s * ROWS, ROWS), ROWS), whole] = (x_v[:, whole].astype(F32) + y).astype(BF16)
                 tiles(body)
-            out_store(s).start()
 
         def attend(i, h):
-            q = jnp.concatenate([qkv[0, h, pl.ds(pl.multiple_of(d * BLOCK + i * ROWS, ROWS), ROWS), :] for d in range(TP)], axis=0)
+            q = jnp.concatenate([q_ref[h, pl.ds(pl.multiple_of(d * BLOCK + i * ROWS, ROWS), ROWS), :] for d in range(TP)], axis=0)
             dims = (((1,), (1,)), ((), ()))
 
             def scores(j):
-                return lax.dot_general(q[j * ROWS:], qkv[1, h, j * BLOCK:(j + 1) * BLOCK, :], dims, preferred_element_type=F32)
+                return lax.dot_general(q[j * ROWS:], k_ref[h, j * BLOCK:(j + 1) * BLOCK, :], dims, preferred_element_type=F32)
 
             row = lax.broadcasted_iota(jnp.int32, (ROWS, BLOCK), 0) + i * ROWS
             keep_mask = lax.broadcasted_iota(jnp.int32, (ROWS, BLOCK), 1) <= row
@@ -401,7 +390,7 @@
                 part = p[:, 0:128]
                 for c in range(1, BLOCK // 128):
                     part = part + p[:, c * 128:(c + 1) * 128]
-                pv = jnp.dot(p.astype(BF16), qkv[2, h, j * BLOCK:(j + 1) * BLOCK, :], preferred_element_type=F32)
+                pv = jnp.dot(p.astype(BF16), v_ref[h, j * BLOCK:(j + 1) * BLOCK, :], preferred_element_type=F32)
                 if j == 0:
                     l, acc = part, pv
                 else:
@@ -456,7 +445,6 @@
         for s in (STEPS - 2, STEPS - 1):
             for half in range(2):
                 hop(s1, s, half).wait_send()
-            out_store(s).wait()
         for s in range(STEPS):
             for half in range(2):
                 for n in range(2):
@@ -470,8 +458,7 @@
                   pltpu.VMEM((2, 2 * ROWS, HALF), F32),
                   pltpu.VMEM((2, 2, ROWS, HALF), BF16),
                   pltpu.VMEM((2, 2, ROWS, HALF), F32),
-                  pltpu.VMEM((ROWS, WIDTH), BF16),
-                  pltpu.VMEM((2, ROWS, WIDTH), BF16))
+                  pltpu.VMEM((ROWS, WIDTH), BF16))
     for p in range(PIECES):
         own(p, 0, XN).wait_send()
         own(p, 1, YN).wait_send()
@@ -484,8 +471,6 @@
     for half in range(2):
         for c in range(WO_PARTS):
             wo_part(c, half).wait_send()
-    v_store().wait()
-    k_store().wait()
 
 
 def block_call(x, an, wq, wk, wv, qg, kg, wo, table):
@@ -494,26 +479,26 @@
     dma = pltpu.SemaphoreType.DMA
     return pl.pallas_call(
         block_kernel,
-        out_shape=[jax.ShapeDtypeStruct((BLOCK, WIDTH), BF16),
-                   jax.ShapeDtypeStruct((HEADS, SEQ, HEAD_DIM), BF16),
-                   jax.ShapeDtypeStruct((HEADS, SEQ, HEAD_DIM), BF16),
+        out_shape=[pltpu.VMEM((BLOCK, WIDTH), BF16),
+                   pltpu.VMEM((HEADS, SEQ, HEAD_DIM), BF16),
+                   pltpu.VMEM((HEADS, SEQ, HEAD_DIM), BF16),
                    jax.ShapeDtypeStruct((TP, BLOCK, WIDTH), BF16)],
         in_specs=[any_spec, vmem_spec, any_spec, any_spec, any_spec, vmem_spec, vmem_spec, any_spec, any_spec],
-        out_specs=[any_spec] * 4,
+        out_specs=[vmem_spec] * 3 + [any_spec],
         scratch_shapes=[
-            pltpu.VMEM((3, HEADS, SEQ, HEAD_DIM), BF16),
+            pltpu.VMEM((HEADS, SEQ, HEAD_DIM), BF16),
             pltpu.VMEM((64, 128), F32),
             pltpu.VMEM((TP, 64, 128), F32),
             pltpu.VMEM((2, COLS, HALF), BF16),
             pltpu.VMEM((2, STEPS, 2, 2 * ROWS, COLS), BF16),
             pltpu.VMEM((2, 2, 2 * ROWS, HALF), BF16),
             pltpu.VMEM((4, 2, ROWS, HALF), BF16),
-            dma((3,)), dma((2,)), dma((2, 2)), dma((7, PIECES)), dma((7, PIECES)), dma((7,)), dma((7,)), dma(()), dma((2,)),
+            dma((3,)), dma((2,)), dma((2, 2)), dma((7, PIECES)), dma((7, PIECES)), dma((7,)), dma((7,)), dma(()),
             dma((2, WO_PARTS)), dma((2, WO_PARTS)), dma((2,)), dma(()),
-            dma((2, STEPS, 2)), dma((2, STEPS, 2)), dma(()), dma((2,)),
+            dma((2, STEPS, 2)), dma((2, STEPS, 2)), dma(()),
             dma(()), dma((2,)), dma((2, 2)), dma((4, 2)),
         ],
-        compiler_params=pltpu.CompilerParams(collective_id=0, has_side_effects=True, vmem_limit_bytes=67043328),
+        compiler_params=pltpu.CompilerParams(collective_id=0, has_side_effects=True, vmem_limit_bytes=48 * 2**20),
         name="block",
     )(x, an, wq, wk, wv, qg, kg, wo, table)
 

time: 378 us -> 372 us (0.984)
  local copies, waits for them, and re-layouts: 11.8 us -> 7.08 us
    unnamed x9 -> x3, local copies, waits for them, and re-layouts: 11.8 us -> 7.08 us
where the time goes in v4:
time: 372 us
  Pallas kernels  364 us (98%)
  local copies, waits for them, and re-layouts  7.08 us (2%)
    pallas_call x1, Pallas kernels, block_call(): pl.pallas_call(block_kernel, out_shape=[pltpu.VMEM((BLOCK, WIDTH), BF16),...  364 us

profile of v4, /device:TPU:0, one launch (start us, length us, event | category | flops | bytes accessed | tf_op | source)
XLA Modules:
  0.0 371.9 jit_solution(2033918378831738040)
XLA Ops:
  0.6 364.2 %block.1 = (bf16[512,5120]{1,0:T(8,128)(2,1)S(1)}, bf16[5,4096,128]{2,1,0:T(8,128)(2,1)S(1)}, bf16[5,4096,128]{2,1,0:T(8,128)(2,1)S(1)}, bf16[8,512,5120]{2,1,0:T(8,128)(2,1)}) custom-call(bf16[512,5120]{1,0:T(8,128)(2,1)} %bitcast.12, f32[1,5120]{1,0:T(1,128)} %bitcast.13, bf16[5120,640]{1,0:T(8,128)(2,1)} %wq_ref.1, bf16[5120,640]{1,0:T(8,128)(2,1)} %wk_ref.1, ...), custom_call_target="tpu_custom_call" | custom-call | tf_op jit(solution)/shard_map/block/pallas_call | solution.py:480
  364.8 2.4 copy.15
  367.2 2.4 copy.16
  369.5 2.4 copy.17

commit v5 on v4

--- a/solution.py
+++ b/solution.py
@@ -24,8 +24,8 @@
 HALF = WIDTH // 2
 TILE = 512
 LAG = 4
-EARLY = 2
-WO_PARTS = 10
+EARLY = 1
+WO_PARTS = 5
 WO_ROWS = COLS // WO_PARTS
 F32 = jnp.float32
 BF16 = jnp.bfloat16
@@ -503,6 +503,33 @@
     )(x, an, wq, wk, wv, qg, kg, wo, table)
 
 
+def write_out(*refs):
+    srcs, dsts, sems = refs[:3], refs[3:6], refs[6]
+    parts = 4
+    copies = []
+    for n, (src, dst) in enumerate(zip(srcs, dsts)):
+        size = src.shape[-2] // parts
+        for p in range(parts):
+            at = (slice(None),) * (len(src.shape) - 2) + (pl.ds(p * size, size),)
+            copies.append(pltpu.make_async_copy(src.at[at], dst.at[at], sems.at[n, p]))
+    for c in copies:
+        c.start()
+    for c in copies:
+        c.wait()
+
+
+def write_out_call(*arrays):
+    return pl.pallas_call(
+        write_out,
+        out_shape=[jax.ShapeDtypeStruct(a.shape, a.dtype) for a in arrays],
+        in_specs=[pl.BlockSpec(memory_space=pltpu.VMEM)] * 3,
+        out_specs=[pl.BlockSpec(memory_space=pl.ANY)] * 3,
+        scratch_shapes=[pltpu.SemaphoreType.DMA((3, 4))],
+        compiler_params=pltpu.CompilerParams(vmem_limit_bytes=2**20),
+        name="write_out",
+    )(*[pltpu.with_memory_space_constraint(a, pltpu.VMEM) for a in arrays])
+
+
 def rope_table():
     half = HEAD_DIM // 2
     freq = (10000.0 ** (-np.arange(half, dtype=np.float64) * (2.0 / HEAD_DIM))).astype(np.float32)
@@ -515,6 +542,7 @@
 
     def local_block(x_local, attn_gain, wq, wk, wv, q_gain, k_gain, wo):
         out, k, v, _ = block_call(x_local[0], attn_gain[None], wq, wk, wv, q_gain, k_gain, wo, jnp.asarray(table))
+        out, k, v = write_out_call(out, k, v)
         k_cache = jnp.transpose(k, (1, 0, 2))[None]
         v_cache = jnp.transpose(v, (1, 0, 2))[None]
         return out[None], k_cache, v_cache

time: 372 us -> 371 us (level)
  local copies, waits for them, and re-layouts: 7.08 us -> 0 us
  Pallas kernels: 364 us -> 370 us
    unnamed x3 -> x0, local copies, waits for them, and re-layouts: 7.08 us -> none
    pallas_call x0 -> x1, Pallas kernels: none -> 5.65 us  [write_out_call(): pl.pallas_call(write_out, out_shape=[jax.ShapeDtypeStruct(a.shape, a.dtyp...]
where the time goes in v5:
time: 371 us; the launch traced here: 370 us
  Pallas kernels  370 us (100%)
    pallas_call x1, Pallas kernels, block_call(): pl.pallas_call(block_kernel, out_shape=[pltpu.VMEM((BLOCK, WIDTH), BF16),...  364 us

profile of v5, /device:TPU:0, one launch (start us, length us, event | category | flops | bytes accessed | tf_op | source)
XLA Modules:
  0.0 370.2 jit_solution(8216327798296357079)
XLA Ops:
  0.6 364.0 %block.1 = (bf16[512,5120]{1,0:T(8,128)(2,1)S(1)}, bf16[5,4096,128]{2,1,0:T(8,128)(2,1)S(1)}, bf16[5,4096,128]{2,1,0:T(8,128)(2,1)S(1)}, bf16[8,512,5120]{2,1,0:T(8,128)(2,1)}) custom-call(bf16[512,5120]{1,0:T(8,128)(2,1)} %bitcast.9, f32[1,5120]{1,0:T(1,128)} %bitcast.10, bf16[5120,640]{1,0:T(8,128)(2,1)} %wq_ref.1, bf16[5120,640]{1,0:T(8,128)(2,1)} %wk_ref.1, ...), custom_call_target="tpu_custom_call" | custom-call | tf_op jit(solution)/shard_map/block/pallas_call | solution.py:480
  364.6 5.6 %write_out.1 = (bf16[512,5120]{1,0:T(8,128)(2,1)}, bf16[5,4096,128]{2,1,0:T(8,128)(2,1)}, bf16[5,4096,128]{2,1,0:T(8,128)(2,1)}) custom-call(bf16[512,5120]{1,0:T(8,128)(2,1)S(1)} %get-tuple-element.9.refs_0_, bf16[5,4096,128]{2,1,0:T(8,128)(2,1)S(1)} %get-tuple-element.10.refs_1_, bf16[5,4096,128]{2,1,0:T(8,128)(2,1)S(1)} %get-tuple-element.11.refs_2_), custom_call_target="tpu_custom_call" | custom-call | tf_op jit(solution)/shard_map/write_out/pallas_call | solution.py:522

commit v6 on v5

--- a/solution.py
+++ b/solution.py
@@ -71,8 +71,8 @@
 
 
 def block_kernel(x_ref, an_ref, wq_ref, wk_ref, wv_ref, qg_ref, kg_ref, wo_ref, tab_ref, out_ref, k_ref, v_ref, hbuf,
-                 q_ref, ssq_v, ssq_all, wr, o_in, recv0, r1,
-                 w_sem, h_sem, n_sem, send_sem, recv_sem, ss_send, ss_recv, ss_loc,
+                 q_ref, ssq_v, ssq_sib, ssq_all, wr, o_in, recv0, r1,
+                 w_sem, h_sem, n_sem, send_sem, recv_sem, ss_send, ss_recv,
                  wo_send, wo_recv, wo_sem, tab_sem, o_send, o_recv, x_sem, y_send, y_recv, s1_send, s1_recv):
     place = Place()
     scale = float(HEAD_DIM ** -0.5 * np.log2(np.e))
@@ -106,11 +106,16 @@
         return remote(wo_ref.at[rows, pl.ds(half * HALF, HALF)], wr.at[half, rows],
                       wo_send.at[half, c], wo_recv.at[half, c], (XN, YN)[half])
 
+    def pair():
+        return remote(ssq_v, ssq_sib, ss_send.at[SIB], ss_recv.at[SIB], SIB)
+
     def share(k):
-        return remote(ssq_v, ssq_all.at[place.me], ss_send.at[k], ss_recv.at[k], k)
+        chip = place.me // 2
+        return remote(ssq_all.at[chip], ssq_all.at[chip], ss_send.at[k], ss_recv.at[k], k)
 
     def shared(k):
-        return remote(ssq_v, ssq_all.at[place.kind(k)], ss_send.at[k], ss_recv.at[k], k)
+        chip = place.kind(k) // 2
+        return remote(ssq_all.at[chip], ssq_all.at[chip], ss_send.at[k], ss_recv.at[k], k)
 
     qkv = (q_ref, k_ref, v_ref)
 
@@ -239,10 +244,11 @@
 
     pl.run_scoped(project_phase, pltpu.VMEM((3, WIDTH, COLS), BF16), pltpu.VMEM((2, UNIT, WIDTH), BF16))
 
-    for k in range(7):
+    pair().start()
+    pair().wait_recv()
+    ssq_all[place.me // 2] = ssq_v[...] + ssq_sib[...]
+    for k in (XN, YN, DG):
         share(k).start()
-    mine = pltpu.make_async_copy(ssq_v, ssq_all.at[place.me], ss_loc)
-    mine.start()
     for c in range(EARLY, WO_PARTS):
         for half in range(2):
             wo_part(c, half).start()
@@ -268,8 +274,7 @@
 
         for half in range(2):
             wo_load(half).start()
-        mine.wait()
-        for k in range(7):
+        for k in (XN, YN, DG):
             shared(k).wait_recv()
         tab.wait()
         low = lax.broadcasted_iota(jnp.int32, (128, 128), 1) < 64
@@ -466,7 +471,8 @@
         for f in forwards(p):
             relay(*f).wait_send()
         relay(DG, p, 6, SDG, SIB).wait_send()
-    for k in range(7):
+    pair().wait_send()
+    for k in (XN, YN, DG):
         share(k).wait_send()
     for half in range(2):
         for c in range(WO_PARTS):
@@ -488,12 +494,13 @@
         scratch_shapes=[
             pltpu.VMEM((HEADS, SEQ, HEAD_DIM), BF16),
             pltpu.VMEM((64, 128), F32),
-            pltpu.VMEM((TP, 64, 128), F32),
+            pltpu.VMEM((64, 128), F32),
+            pltpu.VMEM((TP // 2, 64, 128), F32),
             pltpu.VMEM((2, COLS, HALF), BF16),
             pltpu.VMEM((2, STEPS, 2, 2 * ROWS, COLS), BF16),
             pltpu.VMEM((2, 2, 2 * ROWS, HALF), BF16),
             pltpu.VMEM((4, 2, ROWS, HALF), BF16),
-            dma((3,)), dma((2,)), dma((2, 2)), dma((7, PIECES)), dma((7, PIECES)), dma((7,)), dma((7,)), dma(()),
+            dma((3,)), dma((2,)), dma((2, 2)), dma((7, PIECES)), dma((7, PIECES)), dma((4,)), dma((4,)),
             dma((2, WO_PARTS)), dma((2, WO_PARTS)), dma((2,)), dma(()),
             dma((2, STEPS, 2)), dma((2, STEPS, 2)), dma(()),
             dma(()), dma((2,)), dma((2, 2)), dma((4, 2)),

time: 371 us -> 369 us (level)
  no operation moved by 1% of the time
where the time goes in v6:
time: 369 us
  Pallas kernels  368 us (100%)
    pallas_call x1, Pallas kernels, block_call(): pl.pallas_call(block_kernel, out_shape=[pltpu.VMEM((BLOCK, WIDTH), BF16),...  362 us

profile of v6, /device:TPU:0, one launch (start us, length us, event | category | flops | bytes accessed | tf_op | source)
XLA Modules:
  0.0 368.8 jit_solution(16690069413303865098)
XLA Ops:
  0.6 362.5 %block.1 = (bf16[512,5120]{1,0:T(8,128)(2,1)S(1)}, bf16[5,4096,128]{2,1,0:T(8,128)(2,1)S(1)}, bf16[5,4096,128]{2,1,0:T(8,128)(2,1)S(1)}, bf16[8,512,5120]{2,1,0:T(8,128)(2,1)}) custom-call(bf16[512,5120]{1,0:T(8,128)(2,1)} %bitcast.9, f32[1,5120]{1,0:T(1,128)} %bitcast.10, bf16[5120,640]{1,0:T(8,128)(2,1)} %wq_ref.1, bf16[5120,640]{1,0:T(8,128)(2,1)} %wk_ref.1, ...), custom_call_target="tpu_custom_call" | custom-call | tf_op jit(solution)/shard_map/block/pallas_call | solution.py:486
  363.1 5.6 %write_out.1 = (bf16[512,5120]{1,0:T(8,128)(2,1)}, bf16[5,4096,128]{2,1,0:T(8,128)(2,1)}, bf16[5,4096,128]{2,1,0:T(8,128)(2,1)}) custom-call(bf16[512,5120]{1,0:T(8,128)(2,1)S(1)} %get-tuple-element.9.refs_0_, bf16[5,4096,128]{2,1,0:T(8,128)(2,1)S(1)} %get-tuple-element.10.refs_1_, bf16[5,4096,128]{2,1,0:T(8,128)(2,1)S(1)} %get-tuple-element.11.refs_2_), custom_call_target="tpu_custom_call" | custom-call | tf_op jit(solution)/shard_map/write_out/pallas_call | solution.py:529
